TPU v7x, 32 devices: a whole 2x2x4 slice. The times are simulated.
32 devices in a mesh: groups: 2 (over x), tm: 8 (over z, y), sector: 2 (over core).
Axes of the slice: x: 2, y: 2, z: 4, core: 2. Of those that a mesh axis runs over, the one named last changes fastest.
Arguments:
- context: bfloat16 [16, 2, 512, 256], P(('groups', 'tm'), 'sector'), parts along dimension 0, may hold values from -6 to 6
- depth_weight: float32 [16, 2, 16, 512], P(('groups', 'tm'), 'sector'), parts along dimension 0, may hold values from 0 to 1
- cell_ids: int32 [2, 16, 512], P('sector'), may hold values from 0 to 4095
- time_embed: bfloat16 [8, 256], replicated, may hold values from -3 to 3
- norm_gain: float32 [2, 2, 256], replicated, may hold values from 0.1 to 1.9
- w_qkv: bfloat16 [2, 256, 768], replicated, may hold values from -15 to 15
- w_out: bfloat16 [2, 256, 256], replicated, may hold values from -0.375 to 0.375
- w_up: bfloat16 [2, 256, 1024], replicated, may hold values from -0.375 to 0.375
- w_down: bfloat16 [2, 1024, 256], replicated, may hold values from -0.1875 to 0.1875
- conv_weight: bfloat16 [3, 3, 256, 256], replicated, may hold values from -0.125 to 0.125
Outputs:
- bev_out: bfloat16 [16, 64, 64, 256], P(('groups', 'tm'), 'sector'), parts along dimension 0
There are 2 independent parts, one for each index of `groups`. A program takes and returns all parts, laid end to end along the dimension named above; an argument that names none is the same for every part. Nothing has to cross between parts.
All inputs are finite; a program needn't handle non-finite values.
Results may differ from a plain program's by a relative error of at most 0.0079.
Values may be sent and summed in bfloat16 or wider, within the bound.
No kernel may reach another device: no remote copies, remote signals or barrier semaphores. Data moves between devices by JAX's collectives and lax.ppermute only.
A program may use at most 128 MiB of HBM per device.

v0:
```python
import functools
import math

import jax
import jax.numpy as jnp
from jax import lax
from jax.experimental import pallas as pl
from jax.experimental.pallas import tpu as pltpu
from jax.sharding import PartitionSpec as P


HEADS = 8
GRID = 64
LANES = 128
TILE_LANES = 256
SUBLANES = 8
VMEM_LIMIT = 24 << 20
F32 = jnp.float32
BF16 = jnp.bfloat16
NT = (((1,), (1,)), ((), ()))


def mark(weights, ids, col_hot, row_id):
    bins, pixels = weights[0].shape
    wide = (SUBLANES, pixels)
    column = lax.broadcasted_iota(jnp.int32, wide, 0).astype(F32).astype(BF16)
    for s in range(len(weights)):
        rows = lax.div(ids[s][...], GRID)
        cols = (ids[s][...] - rows * GRID).astype(F32)
        rows = rows.astype(F32)
        for d in range(bins):
            row_id[s, d] = jnp.broadcast_to(rows[d : d + 1], wide).astype(BF16)
            col = jnp.broadcast_to(cols[d : d + 1], wide).astype(BF16)
            value = jnp.broadcast_to(weights[s][d : d + 1, :], wide).astype(BF16)
            for j in range(GRID // SUBLANES):
                low = j * SUBLANES
                hit = column + low == col
                col_hot[s, d, low : low + SUBLANES] = jnp.where(
                    hit, value, jnp.zeros_like(value)
                )


def match(place, slot, matrix, base, col_hot, row_id, piece_rows, chunk_order):
    sectors, bins, _, pixels = col_hot.shape
    blocks = pixels // TILE_LANES
    shape = (SUBLANES, TILE_LANES)
    piece = place[0] ^ slot
    for first in range(0, piece_rows, 2):
        targets = []
        for row in chunk_order[first : first + 2]:
            target = (place[1] + piece * piece_rows + row).astype(F32)
            targets.append(jnp.full(shape, target, F32).astype(BF16))

        def step(n, _):
            s = n // blocks
            at = pl.ds(pl.multiple_of((n % blocks) * TILE_LANES, TILE_LANES), TILE_LANES)
            sums = [[jnp.zeros(shape, BF16)] * (GRID // SUBLANES) for _ in targets]
            for d in range(bins):
                row = row_id[s, d, :, at]
                hits = [row == target for target in targets]
                for j in range(GRID // SUBLANES):
                    part = col_hot[s, d, j * SUBLANES : (j + 1) * SUBLANES, at]
                    for k, hit in enumerate(hits):
                        sums[k][j] = sums[k][j] + jnp.where(hit, part, jnp.zeros_like(part))
            for k in range(len(targets)):
                for j in range(GRID // SUBLANES):
                    low = base + (first + k) * GRID + j * SUBLANES
                    matrix[s, low : low + SUBLANES, at] = sums[k][j]
            return 0

        lax.fori_loop(0, sectors * blocks, step, 0)


def multiply(context_t, matrix, low, cells):
    total = None
    for s in range(matrix.shape[0]):
        rows = matrix[s, low : low + cells]
        part = lax.dot_general(context_t[s], rows, NT, preferred_element_type=F32)
        part = part.astype(BF16).astype(F32)
        total = part if total is None else total + part
    return total.astype(BF16)


def pool_kernel(place, *refs, slots, piece_rows, chunk_order):
    *refs, context_t, col_hot, row_id, matrix, context, weight, ids, arrived = refs
    out_refs, refs = refs[-len(slots) :], refs[: -len(slots)]
    held = (context, weight, ids)
    copies = [pltpu.make_async_copy(refs[n], held[n], arrived.at[n]) for n in range(3)]
    for copy in copies:
        copy.start()
    for copy in copies:
        copy.wait()
    refs = held + tuple(refs[3:])
    mark(refs[1::3], refs[2::3], col_hot, row_id)
    for s, context in enumerate(refs[0::3]):
        context_t[s] = context[...].astype(F32).T.astype(BF16)
    for slot, out_ref in zip(slots, out_refs):
        match(place, slot, matrix, 0, col_hot, row_id, piece_rows, chunk_order)
        out_ref[...] = multiply(context_t, matrix, 0, matrix.shape[1])


def match_kernel(place, *refs, slots, piece_rows, chunk_order):
    *refs, matrix, col_hot, row_id = refs
    mark(refs[0::2], refs[1::2], col_hot, row_id)
    cells = piece_rows * GRID
    for n, slot in enumerate(slots):
        match(place, slot, matrix, n * cells, col_hot, row_id, piece_rows, chunk_order)


def multiply_kernel(*refs, sectors):
    contexts, matrix = refs[:sectors], refs[sectors]
    out_refs, context_t = refs[sectors + 1 : -1], refs[-1]
    for s in range(sectors):
        context_t[s] = contexts[s][...].astype(F32).T.astype(BF16)
    cells = matrix.shape[1] // len(out_refs)
    for n, out_ref in enumerate(out_refs):
        out_ref[...] = multiply(context_t, matrix, n * cells, cells)


def hot_scratch(sectors, bins, pixels):
    return [
        pltpu.VMEM((sectors, bins, GRID, pixels), BF16),
        pltpu.VMEM((sectors, bins, SUBLANES, pixels), BF16),
    ]


def pool(place, contexts, depths, ids, slots, piece_rows, chunk_order):
    pixels, channels = contexts[0].shape
    bins = depths[0].shape[0]
    sectors = len(contexts)
    cells = piece_rows * GRID
    vmem = pl.BlockSpec(memory_space=pltpu.VMEM)
    return pl.pallas_call(
        functools.partial(
            pool_kernel, slots=slots, piece_rows=piece_rows, chunk_order=chunk_order
        ),
        out_shape=[jax.ShapeDtypeStruct((channels, cells), BF16)] * len(slots),
        in_specs=[pl.BlockSpec(memory_space=pltpu.SMEM)]
        + [pl.BlockSpec(memory_space=pltpu.HBM)] * 3
        + [vmem] * (3 * sectors - 3),
        out_specs=[vmem] * len(slots),
        scratch_shapes=[pltpu.VMEM((sectors, channels, pixels), BF16)]
        + hot_scratch(sectors, bins, pixels)
        + [pltpu.VMEM((sectors, cells, pixels), BF16)]
        + [pltpu.VMEM(a.shape, a.dtype) for a in (contexts[0], depths[0], ids[0])]
        + [pltpu.SemaphoreType.DMA((3,))],
        compiler_params=pltpu.CompilerParams(vmem_limit_bytes=VMEM_LIMIT),
        cost_estimate=pl.CostEstimate(
            flops=2 * sectors * len(slots) * cells * pixels * channels,
            bytes_accessed=2 * len(slots) * cells * channels,
            transcendentals=0,
        ),
        name="pool",
    )(place, *[a for args in zip(contexts, depths, ids) for a in args])


def pool_matrix(place, depths, ids, slots, piece_rows, chunk_order):
    bins, pixels = depths[0].shape
    sectors = len(depths)
    cells = piece_rows * GRID
    vmem = pl.BlockSpec(memory_space=pltpu.VMEM)
    return pl.pallas_call(
        functools.partial(
            match_kernel, slots=slots, piece_rows=piece_rows, chunk_order=chunk_order
        ),
        out_shape=jax.ShapeDtypeStruct((sectors, len(slots) * cells, pixels), BF16),
        in_specs=[pl.BlockSpec(memory_space=pltpu.SMEM)] + [vmem] * (2 * sectors),
        out_specs=vmem,
        scratch_shapes=hot_scratch(sectors, bins, pixels),
        compiler_params=pltpu.CompilerParams(vmem_limit_bytes=VMEM_LIMIT),
        cost_estimate=pl.CostEstimate(
            flops=2 * sectors * len(slots) * cells * pixels * bins,
            bytes_accessed=2 * len(slots) * cells * pixels,
            transcendentals=0,
        ),
        name="pool_matrix",
    )(place, *[a for args in zip(depths, ids) for a in args])


def pool_multiply(contexts, matrix, count):
    pixels, channels = contexts[0].shape
    cells = matrix.shape[1] // count
    vmem = pl.BlockSpec(memory_space=pltpu.VMEM)
    return pl.pallas_call(
        functools.partial(multiply_kernel, sectors=len(contexts)),
        out_shape=[jax.ShapeDtypeStruct((channels, cells), BF16)] * count,
        in_specs=[vmem] * (len(contexts) + 1),
        out_specs=[vmem] * count,
        scratch_shapes=[pltpu.VMEM((len(contexts), channels, pixels), BF16)],
        compiler_params=pltpu.CompilerParams(vmem_limit_bytes=VMEM_LIMIT),
        cost_estimate=pl.CostEstimate(
            flops=2 * matrix.size * channels,
            bytes_accessed=2 * matrix.size,
            transcendentals=0,
        ),
        name="pool_multiply",
    )(*contexts, matrix)


def prep_kernel(w_qkv, w_out, w_up, w_down, gain, embed, qkv_t, out_t, up_t, down_t, gains, embeds):
    _, channels, _ = w_qkv.shape
    hidden = w_up.shape[2]
    size = channels // HEADS
    row = lax.broadcasted_iota(jnp.int32, (channels, channels), 0)
    col = lax.broadcasted_iota(jnp.int32, (channels, channels), 1)
    order = (col == (row % HEADS) * size + row // HEADS).astype(F32).astype(BF16)
    same = (col == row).astype(F32).astype(BF16)

    def turned(left, right):
        return lax.dot_general(left, right, NT, preferred_element_type=F32).astype(BF16)

    def columns(values):
        return jnp.broadcast_to(values, (LANES, channels)).T

    for j in range(3):
        at = slice(j * channels, (j + 1) * channels)
        qkv_t[0, at, :] = turned(order, w_qkv[0, :, at])
    rows = jnp.dot(order, w_out[0], preferred_element_type=F32).astype(BF16)
    out_t[0] = turned(same, rows)
    for j in range(0, hidden, channels):
        at = slice(j, j + channels)
        up_t[0, at, :] = turned(same, w_up[0, :, at])
        down_t[0, :, at] = turned(same, w_down[0, at, :])
    for k in range(gain.shape[1]):
        gains[0, k] = columns(gain[0, k : k + 1, :])

    @pl.when(pl.program_id(0) == 0)
    def _():
        for f in range(embed.shape[0]):
            embeds[f] = columns(embed[f : f + 1, :].astype(F32))


def prep(w_qkv, w_out, w_up, w_down, norm_gain, time_embed):
    matrices = (w_qkv, w_out, w_up, w_down)
    channels = time_embed.shape[1]
    a_layer = lambda shape: pl.BlockSpec((1,) + shape[1:], lambda l: (l,) + (0,) * (len(shape) - 1))
    whole = lambda shape: pl.BlockSpec(shape, lambda l: (0,) * len(shape))
    gains = norm_gain.shape + (LANES,)
    embeds = time_embed.shape + (LANES,)
    turned = [(w.shape[0], w.shape[2], w.shape[1]) for w in matrices]
    return pl.pallas_call(
        prep_kernel,
        grid=(w_qkv.shape[0],),
        out_shape=[jax.ShapeDtypeStruct(shape, BF16) for shape in turned]
        + [jax.ShapeDtypeStruct(gains, F32), jax.ShapeDtypeStruct(embeds, F32)],
        in_specs=[a_layer(w.shape) for w in matrices]
        + [a_layer(norm_gain.shape), whole(time_embed.shape)],
        out_specs=[a_layer(shape) for shape in turned] + [a_layer(gains), whole(embeds)],
        compiler_params=pltpu.CompilerParams(
            dimension_semantics=("arbitrary",), vmem_limit_bytes=VMEM_LIMIT
        ),
        cost_estimate=pl.CostEstimate(
            flops=2 * channels * sum(w.size for w in matrices),
            bytes_accessed=4 * sum(w.size for w in matrices),
            transcendentals=0,
        ),
        name="prep",
    )(*matrices, norm_gain, time_embed)


def normed_tile(stream, gain):
    mean = jnp.mean(stream * stream, axis=0, keepdims=True)
    scale = lax.rsqrt(mean + 1e-05)
    lanes = stream.shape[1]
    gains = jnp.concatenate([gain] * (lanes // LANES), axis=1)
    return (stream * scale * gains).astype(BF16)


def gelu(values):
    root = (2.0 / math.pi) ** 0.5
    values = values.astype(BF16)
    half = 0.5 * values
    return half + half * jnp.tanh(values * (root + (root * 0.044715) * (values * values)))


def query_groups(frames, most):
    groups, group, pairs = [], [], 0
    for f in range(frames):
        if group and pairs + f + 1 > most:
            groups.append(group)
            group, pairs = [], 0
        group.append(f)
        pairs += f + 1
    return groups + [group]


def attention(qkv, mixed, frames, cells, channels):
    size = channels // HEADS
    for group in query_groups(frames, 40):
        last = group[-1]
        for lane in range(0, cells, LANES):
            pairs = [(f, g) for f in group for g in range(f + 1)]

            def at(f):
                return slice(f * cells + lane, f * cells + lane + LANES)

            def score_step(d, sums):
                row = pl.multiple_of(d * HEADS, HEADS)
                query = {f: qkv[pl.ds(row, HEADS), at(f)] for f in group}
                keys = [qkv[pl.ds(channels + row, HEADS), at(g)] for g in range(last + 1)]
                return tuple(s + query[f] * keys[g] for s, (f, g) in zip(sums, pairs))

            zeros = tuple(jnp.zeros((HEADS, LANES), F32) for _ in pairs)
            scores = dict(zip(pairs, lax.fori_loop(0, size, score_step, zeros, unroll=4)))
            weights = {}
            for f in group:
                row = [scores[f, g] for g in range(f + 1)]
                largest = functools.reduce(jnp.maximum, row)
                raised = [jnp.exp((s - largest) * size ** (-0.5)) for s in row]
                share = 1.0 / functools.reduce(jnp.add, raised)
                for g in range(f + 1):
                    weights[f, g] = (raised[g] * share).astype(BF16).astype(F32)

            def mix_step(step, carry):
                parts = {f: [] for f in group}
                for half in range(2):
                    row = pl.multiple_of(2 * channels + (2 * step + half) * HEADS, HEADS)
                    values = [qkv[pl.ds(row, HEADS), at(g)] for g in range(last + 1)]
                    for f in group:
                        terms = [carry[pairs.index((f, g))] * values[g] for g in range(f + 1)]
                        parts[f].append(functools.reduce(jnp.add, terms))
                low = pl.multiple_of(step * 2 * HEADS, 2 * HEADS)
                for f in group:
                    mixed[pl.ds(low, 2 * HEADS), at(f)] = jnp.concatenate(
                        parts[f], axis=0
                    ).astype(BF16)
                return carry

            lax.fori_loop(
                0, size // 2, mix_step, tuple(weights[pair] for pair in pairs), unroll=2
            )


def encode_kernel(place, *refs, slots, chunk, cells, valid, last, tile):
    *refs, stream, qkv, mixed = refs
    tokens, refs = refs[:slots], refs[slots:]
    embed, gains, qkv_t, out_t, up_t, down_t, *outs = refs
    half = slots // 2
    layers, _, channels = qkv_t.shape
    lanes = slots * cells
    for k in range(slots):
        frame = place[0] ^ k
        for lane in range(0, cells, LANES):
            at = pl.ds(pl.multiple_of(frame * cells + lane, LANES), LANES)
            low = chunk * cells + lane
            stream[:, at] = tokens[k][:, low : low + LANES].astype(F32) + embed[frame]

    def layer(l, _):
        def project(t, _):
            at = pl.ds(pl.multiple_of(t * tile, tile), tile)
            normed = normed_tile(stream[:, at], gains[l, 0])
            out = jnp.dot(qkv_t[l], normed, preferred_element_type=F32)
            qkv[:, at] = out.astype(BF16).astype(F32)
            return 0

        lax.fori_loop(0, lanes // tile, project, 0, unroll=2)
        attention(qkv, mixed, slots, cells, channels)

        def feed(t, _):
            at = pl.ds(pl.multiple_of(t * tile, tile), tile)
            current = stream[:, at] + jnp.dot(
                out_t[l], mixed[:, at], preferred_element_type=F32
            )
            normed = normed_tile(current, gains[l, 1])
            up = jnp.dot(up_t[l], normed, preferred_element_type=F32)
            hidden = gelu(up)
            stream[:, at] = current + jnp.dot(down_t[l], hidden, preferred_element_type=F32)
            return 0

        lax.fori_loop(0, lanes // tile, feed, 0, unroll=2)
        return 0

    lax.fori_loop(0, layers, layer, 0)
    earlier, outs = outs[:chunk] if last else [], outs[chunk:] if last else outs
    for k in range(slots):
        at = pl.ds(pl.multiple_of((place[0] ^ k) * cells, LANES), cells)
        done = stream[:, at].T.astype(BF16)[:valid]
        if not last:
            outs[k // half][k % half] = done
        elif k >= half:
            outs[k][...] = done
        else:
            for c, before in enumerate(earlier):
                outs[k][c * valid : (c + 1) * valid] = before[k]
            outs[k][chunk * valid : (chunk + 1) * valid] = done


def encode(place, tokens, weights, gains, embed, earlier, chunk, chunks):
    slots = len(tokens)
    half = slots // 2
    channels, piece_cells = tokens[0].shape
    valid = piece_cells // chunks
    spare = -valid % LANES
    if spare:
        tokens = [jnp.pad(t, ((0, 0), (0, spare))) for t in tokens]
    cells = valid + spare
    layers, hidden = weights[2].shape[:2]
    lanes = slots * cells
    last = chunk == chunks - 1
    if last:
        shapes = [(chunks * valid, channels)] * half + [(valid, channels)] * half
    else:
        shapes = [(half, valid, channels)] * 2
    vmem = pl.BlockSpec(memory_space=pltpu.VMEM)
    operands = [*tokens, embed, gains, *weights, *(earlier if last else [])]
    return pl.pallas_call(
        functools.partial(
            encode_kernel,
            slots=slots,
            chunk=chunk,
            cells=cells,
            valid=valid,
            last=last,
            tile=min(lanes, 512),
        ),
        out_shape=[jax.ShapeDtypeStruct(shape, BF16) for shape in shapes],
        in_specs=[pl.BlockSpec(memory_space=pltpu.SMEM)] + [vmem] * len(operands),
        out_specs=[vmem] * len(shapes),
        scratch_shapes=[
            pltpu.VMEM((channels, lanes), F32),
            pltpu.VMEM((3 * channels, lanes), F32),
            pltpu.VMEM((channels, lanes), BF16),
        ],
        compiler_params=pltpu.CompilerParams(vmem_limit_bytes=VMEM_LIMIT),
        cost_estimate=pl.CostEstimate(
            flops=2 * layers * lanes * channels * (4 * channels + 2 * hidden),
            bytes_accessed=4 * lanes * channels,
            transcendentals=layers * lanes * hidden,
        ),
        name="encode",
    )(place, *operands)


def edge_kernel(place, *refs, slots, rows, single):
    parts, outs = refs[:slots], refs[slots:]
    for k in range(slots):
        piece = place[0] ^ k
        is_head, is_tail = piece == 0, piece == slots - 1
        if single:
            is_head = jnp.logical_and(is_head, place[1] != 0)
            is_tail = jnp.logical_and(is_tail, place[1] == 0)

        @pl.when(is_head)
        def _():
            outs[0][...] = parts[k][0:GRID]

        @pl.when(is_tail)
        def _():
            outs[-1][...] = parts[k][rows - GRID : rows]


def edges(place, parts, rows, single):
    channels = parts[0].shape[1]
    vmem = pl.BlockSpec(memory_space=pltpu.VMEM)
    count = 1 if single else 2
    return pl.pallas_call(
        functools.partial(edge_kernel, slots=len(parts), rows=rows, single=single),
        out_shape=[jax.ShapeDtypeStruct((GRID, channels), BF16)] * count,
        in_specs=[pl.BlockSpec(memory_space=pltpu.SMEM)] + [vmem] * len(parts),
        out_specs=[vmem] * count,
        compiler_params=pltpu.CompilerParams(vmem_limit_bytes=VMEM_LIMIT),
        name="edges",
    )(place, *parts)


def conv_kernel(place, top, bottom, *refs, layout, chunks, piece_rows, bands, block):
    *parts, weight, out_ref, rows = refs
    slots = len(layout)
    total = slots * piece_rows
    inside = (place[1] > 0, place[1] < (bands - 1) * total)
    for edge, has, low in ((top, inside[0], 0), (bottom, inside[1], (total + 1) * GRID)):
        keep = jnp.full(edge.shape, has.astype(jnp.int32), jnp.int32) > 0
        rows[low : low + GRID] = jnp.where(keep, edge[...].astype(F32), 0.0).astype(BF16)
    for k in range(slots):
        base = (1 + (place[0] ^ k) * piece_rows) * GRID
        for c, chunk in enumerate(chunks):
            source, start = layout[k][c]
            for i, row in enumerate(chunk):
                low = pl.multiple_of(base + row * GRID, GRID)
                first = start + i * GRID
                rows[pl.ds(low, GRID)] = parts[source][first : first + GRID]

    cells = block * GRID
    column = lax.broadcasted_iota(jnp.int32, (cells, 1), 0) % GRID

    def one_block(n, _):
        def taps(j):
            sums = None
            for i in range(3):
                at = pl.ds(pl.multiple_of((n * block + i) * GRID, GRID), cells)
                product = jnp.dot(rows[at], weight[i, j], preferred_element_type=F32)
                sums = product if sums is None else sums + product
            return sums

        at = pl.ds(pl.multiple_of((n * block + 1) * GRID, GRID), cells)
        summed = rows[at].astype(F32) + taps(1)
        summed = summed + jnp.where(column == 0, 0.0, pltpu.roll(taps(0), 1, 0))
        summed = summed + jnp.where(column == GRID - 1, 0.0, pltpu.roll(taps(2), cells - 1, 0))
        out_ref[pl.ds(pl.multiple_of(n * cells, cells), cells)] = summed.astype(BF16)
        return 0

    lax.fori_loop(0, total // block, one_block, 0)


def convolve(place, top, bottom, parts, weight, layout, chunks, bands):
    channels = weight.shape[-1]
    piece_rows = sum(len(chunk) for chunk in chunks)
    total = len(layout) * piece_rows
    vmem = pl.BlockSpec(memory_space=pltpu.VMEM)
    return pl.pallas_call(
        functools.partial(
            conv_kernel,
            layout=layout,
            chunks=chunks,
            piece_rows=piece_rows,
            bands=bands,
            block=math.gcd(total, 8),
        ),
        out_shape=jax.ShapeDtypeStruct((total * GRID, channels), BF16),
        in_specs=[pl.BlockSpec(memory_space=pltpu.SMEM)] + [vmem] * (len(parts) + 3),
        out_specs=vmem,
        scratch_shapes=[pltpu.VMEM(((total + 2) * GRID, channels), BF16)],
        compiler_params=pltpu.CompilerParams(vmem_limit_bytes=VMEM_LIMIT),
        cost_estimate=pl.CostEstimate(
            flops=2 * total * GRID * weight.size,
            bytes_accessed=4 * total * GRID * channels,
            transcendentals=0,
        ),
        name="convolve",
    )(place, top, bottom, *parts, weight)


def row_chunks(piece_rows):
    if piece_rows % 4:
        return (tuple(range(piece_rows)),)
    quarter = piece_rows // 4
    inner = tuple(range(quarter, 3 * quarter))
    outer = tuple(range(quarter)) + tuple(range(3 * quarter, piece_rows))
    return (outer, inner)


def body(
    context, depth_weight, cell_ids, time_embed, norm_gain, w_qkv, w_out, w_up, w_down, conv_weight
):
    sectors = lax.axis_size("sector")
    slots = lax.axis_size("tm")
    half = slots // 2
    if context.shape[0] != 1 or slots & (slots - 1):
        raise ValueError("unsupported mesh")
    band_rows = GRID // sectors
    piece_rows = band_rows // slots
    chunks = row_chunks(piece_rows)
    valid = piece_rows * GRID // len(chunks)
    band = lax.axis_index("sector").astype(jnp.int32)
    place = jnp.stack([lax.axis_index("tm").astype(jnp.int32), band * band_rows])

    def from_others(value):
        values = [value]
        for shift in range(1, sectors):
            ring = [(i, (i + shift) % sectors) for i in range(sectors)]
            values.append(lax.ppermute(value, "sector", ring))
        return values

    def swap(value, k):
        if k == 0:
            return value
        return lax.ppermute(value, "tm", [(i, i ^ k) for i in range(slots)])

    order = (piece_rows, sum(chunks, ()))
    near = tuple(range(half))
    depth = swap(depth_weight[0, 0], half)
    features = swap(context[0, 0], half)
    contexts = from_others(context[0, 0])
    depths = from_others(depth_weight[0, 0])
    ids = from_others(cell_ids[0])
    depths_partner = from_others(depth)
    own = pool(place, contexts, depths, ids, near, *order)
    tokens = [swap(own[k], k) for k in near]
    matrix = pool_matrix(place, depths_partner, ids, near, *order)
    contexts = from_others(features)
    partner = pool_multiply(contexts, matrix, half)
    tokens += [swap(partner[k], k) for k in near]
    *weights, gains, embed = prep(w_qkv, w_out, w_up, w_down, norm_gain, time_embed)

    earlier, crossed = [], []
    for c in range(len(chunks) - 1):
        near_part, far_part = encode(place, tokens, weights, gains, embed, [], c, len(chunks))
        earlier.append(near_part)
        crossed.append(swap(far_part, half))
    outs = encode(
        place, tokens, weights, gains, embed, earlier, len(chunks) - 1, len(chunks)
    )
    parts, layout = [], [[None] * len(chunks) for _ in range(slots)]

    for k in range(half, slots):
        parts.append(swap(outs[k], k))
        layout[k][-1] = (len(parts) - 1, 0)
    for k in near:
        parts.append(swap(outs[k], k))
        for c in range(len(chunks)):
            layout[k][c] = (len(parts) - 1, c * valid)
    for c, received in enumerate(crossed):
        for k in near:
            parts.append(swap(received[k], k))
            layout[half + k][c] = (len(parts) - 1, 0)

    first = [parts[layout[k][0][0]] for k in range(slots)]
    up = [(i, i + 1) for i in range(sectors - 1)]
    down = [(i + 1, i) for i in range(sectors - 1)]
    if sectors == 2:
        (edge,) = edges(place, first, valid, True)
        top = bottom = lax.ppermute(edge, "sector", up + down)
    else:
        head, tail = edges(place, first, valid, False)
        top, bottom = lax.ppermute(tail, "sector", up), lax.ppermute(head, "sector", down)
    out = convolve(place, top, bottom, parts, conv_weight, layout, chunks, sectors)
    return out.reshape(1, band_rows, GRID, -1)


def solution(mesh):
    return jax.shard_map(
        body,
        mesh=mesh,
        in_specs=(
            P(("groups", "tm"), "sector", None, None),
            P(("groups", "tm"), "sector", None, None),
            P("sector", None, None),
            P(),
            P(),
            P(),
            P(),
            P(),
            P(),
            P(),
        ),
        out_specs=P(("groups", "tm"), "sector", None, None),
        check_vma=False,
    )
```

profile of v0, /device:TPU:0, one launch (start us, length us, event | category | flops | bytes accessed | tf_op | source)
XLA Modules:
  0.0 98.7 jit_solution(1875504190916472304)
XLA Ops:
  0.0 4.1 %collective-permute-start.6 = (bf16[512,256]{1,0:T(8,128)(2,1)}, bf16[512,256]{1,0:T(8,128)(2,1)S(1)}, u32[]{:S(2)}, u32[]{:S(2)}) collective-permute-start(bf16[512,256]{1,0:T(8,128)(2,1)} %bitcast.17), channel_id=1, source_target_pairs={{0,8},{2,10},{4,12},{6,14},{8,0},{10,2},{12,4},{14,6},{1,9},{3,11}... | collective-permute-start | bytes 786440 | tf_op jit(solution)/shard_map/ppermute | solution.py:567
  4.1 12.1 %collective-permute-done.6.refs_0_ = bf16[512,256]{1,0:T(8,128)(2,1)S(1)} collective-permute-done((bf16[512,256]{1,0:T(8,128)(2,1)}, bf16[512,256]{1,0:T(8,128)(2,1)S(1)}, u32[]{:S(2)}, u32[]{:S(2)}) %collective-permute-start.6) | collective-permute-done | bytes 262176 | tf_op jit(solution)/shard_map/ppermute | solution.py:567
  20.6 5.7 %pool.1 = (bf16[256,256]{1,0:T(8,128)(2,1)S(1)}, bf16[256,256]{1,0:T(8,128)(2,1)S(1)}, bf16[256,256]{1,0:T(8,128)(2,1)S(1)}, bf16[256,256]{1,0:T(8,128)(2,1)S(1)}) custom-call(s32[2]{0:T(128)S(1)} %pad_add_fusion.place, bf16[512,256]{1,0:T(8,128)(2,1)S(1)} %bitcast.19, f32[16,512]{1,0:T(8,128)S(1)} %bitcast.21, s32[16,512]{1,0:T(8,128)S(1)} %bitcast.15, ...), custom_call_target="tpu_custom_call" | custom-call | flops 536870912 | bytes 524288 | tf_op jit(solution)/shard_map/pool/pallas_call | solution.py:133
  26.3 1.6 %collective-permute-start.3 = (bf16[256,256]{1,0:T(8,128)(2,1)S(1)}, bf16[256,256]{1,0:T(8,128)(2,1)S(1)}, u32[]{:S(2)}, u32[]{:S(2)}) collective-permute-start(bf16[256,256]{1,0:T(8,128)(2,1)S(1)} %get-tuple-element.30), channel_id=1, source_target_pairs={{0,2},{2,0},{4,6},{6,4},{8,10},{10,8},{12,14},{14,12},{1,3},{3,1},... | collective-permute-start | bytes 393224 | tf_op jit(solution)/shard_map/ppermute | solution.py:567
  27.9 4.9 %collective-permute-done.8.refs_0_ = f32[16,512]{1,0:T(8,128)S(1)} collective-permute-done((f32[16,512]{1,0:T(8,128)S(1)}, f32[16,512]{1,0:T(8,128)S(1)}, u32[]{:S(2)}, u32[]{:S(2)}) %collective-permute-start.8) | collective-permute-done | bytes 32800 | tf_op jit(solution)/shard_map/ppermute | solution.py:567
  32.9 1.2 %collective-permute-done.9.refs_2_ = f32[16,512]{1,0:T(8,128)S(1)} collective-permute-done((f32[16,512]{1,0:T(8,128)S(1)}, f32[16,512]{1,0:T(8,128)S(1)}, u32[]{:S(2)}, u32[]{:S(2)}) %collective-permute-start.9) | collective-permute-done | bytes 32800 | tf_op jit(solution)/shard_map/ppermute | solution.py:561
  34.8 4.1 %pool_matrix.1.refs_2_ = bf16[2,1024,512]{2,1,0:T(8,128)(2,1)S(1)} custom-call(s32[2]{0:T(128)S(1)} %pad_add_fusion.place, f32[16,512]{1,0:T(8,128)S(1)} %collective-permute-done.8.refs_0_, s32[16,512]{1,0:T(8,128)S(1)} %bitcast.16, f32[16,512]{1,0:T(8,128)S(1)} %collective-permute-done.9.refs_2_, s32[16,512]{1,0:T(8,128)S(1)} %collective-permute-done.2.refs_5_.refs_3_), custom_call_target="tpu_custom_call" | custom-call | flops 33554432 | bytes 1048576 | tf_op jit(solution)/shard_map/pool_matrix/pallas_call | solution.py:162
  41.7 1.6 %collective-permute-start.10 = (bf16[256,256]{1,0:T(8,128)(2,1)S(1)}, bf16[256,256]{1,0:T(8,128)(2,1)S(1)}, u32[]{:S(2)}, u32[]{:S(2)}) collective-permute-start(bf16[256,256]{1,0:T(8,128)(2,1)S(1)} %get-tuple-element.34), channel_id=1, source_target_pairs={{0,2},{2,0},{4,6},{6,4},{8,10},{10,8},{12,14},{14,12},{1,3},{3,1},... | collective-permute-start | bytes 393224 | tf_op jit(solution)/shard_map/ppermute | solution.py:567
  45.3 1.8 %prep.1 = (bf16[2,768,256]{2,1,0:T(8,128)(2,1)S(1)}, bf16[2,256,256]{2,1,0:T(8,128)(2,1)S(1)}, bf16[2,1024,256]{2,1,0:T(8,128)(2,1)S(1)}, bf16[2,256,1024]{2,1,0...) custom-call(bf16[2,256,768]{2,1,0:T(8,128)(2,1)S(1)} %copy-done.2, ...), custom_call_target="tpu_custom_call" | custom-call | flops 805306368 | bytes 6291456 | tf_op jit(solution)/shard_map/prep/pallas_call | solution.py:241
  48.1 1.4 %collective-permute-done.10.refs_5_ = bf16[256,256]{1,0:T(8,128)(2,1)S(1)} collective-permute-done((bf16[256,256]{1,0:T(8,128)(2,1)S(1)}, bf16[256,256]{1,0:T(8,128)(2,1)S(1)}, u32[]{:S(2)}, u32[]{:S(2)}) %collective-permute-start.10) | collective-permute-done | bytes 131104 | tf_op jit(solution)/shard_map/ppermute | solution.py:567
  49.6 1.4 %collective-permute-done.11.refs_6_ = bf16[256,256]{1,0:T(8,128)(2,1)S(1)} collective-permute-done((bf16[256,256]{1,0:T(8,128)(2,1)S(1)}, bf16[256,256]{1,0:T(8,128)(2,1)S(1)}, u32[]{:S(2)}, u32[]{:S(2)}) %collective-permute-start.11) | collective-permute-done | bytes 131104 | tf_op jit(solution)/shard_map/ppermute | solution.py:567
  51.0 1.9 %collective-permute-done.12.refs_7_ = bf16[256,256]{1,0:T(8,128)(2,1)S(1)} collective-permute-done((bf16[256,256]{1,0:T(8,128)(2,1)S(1)}, bf16[256,256]{1,0:T(8,128)(2,1)S(1)}, u32[]{:S(2)}, u32[]{:S(2)}) %collective-permute-start.12) | collective-permute-done | bytes 131104 | tf_op jit(solution)/shard_map/ppermute | solution.py:567
  53.0 7.7 %encode.2 = (bf16[4,128,256]{2,1,0:T(8,128)(2,1)S(1)}, bf16[4,128,256]{2,1,0:T(8,128)(2,1)S(1)}) custom-call(s32[2]{0:T(128)S(1)} %pad_add_fusion.place, bf16[256,256]{1,0:T(8,128)(2,1)S(1)} %get-tuple-element.29.refs_0_, bf16[256,256]{1,0:T(8,128)(2,1)S(1)} %collective-permute-done.3.refs_1_, bf16[256,256]{1,0:T(8,128)(2,1)S(1)} %collective-permute-done.4.refs_2_, ...), custom_call_target="tpu_custom_call" | custom-call | flops 3221225472 | bytes 1048576 | tf_op jit(solution)/shard_map/encode/pallas_call | solution.py:406
  60.7 2.3 %collective-permute-start.16 = (bf16[4,128,256]{2,1,0:T(8,128)(2,1)S(1)}, bf16[4,128,256]{2,1,0:T(8,128)(2,1)S(1)}, u32[]{:S(2)}, u32[]{:S(2)}) collective-permute-start(bf16[4,128,256]{2,1,0:T(8,128)(2,1)S(1)} %get-tuple-element.48), channel_id=1, source_target_pairs={{0,8},{2,10},{4,12},{6,14},{8,0},{10,2},{12,4},{14,6},{1,9},{3,11}... | collective-permute-start | bytes 786440 | tf_op jit(solution)/shard_map/ppermute | solution.py:567
  62.9 7.7 %encode.3 = (bf16[256,256]{1,0:T(8,128)(2,1)S(1)}, bf16[256,256]{1,0:T(8,128)(2,1)S(1)}, bf16[256,256]{1,0:T(8,128)(2,1)S(1)}, bf16[256,256]{1,0:T(8,128)(2,1)S(...) custom-call(s32[2]{0:T(128)S(1)} %pad_add_fusion.place, ...), custom_call_target="tpu_custom_call" | custom-call | flops 3221225472 | bytes 1048576 | tf_op jit(solution)/shard_map/encode/pallas_call | solution.py:406
  70.6 1.6 %collective-permute-start.13 = (bf16[256,256]{1,0:T(8,128)(2,1)S(1)}, bf16[256,256]{1,0:T(8,128)(2,1)S(1)}, u32[]{:S(2)}, u32[]{:S(2)}) collective-permute-start(bf16[256,256]{1,0:T(8,128)(2,1)S(1)} %get-tuple-element.45), channel_id=1, source_target_pairs={{0,2},{2,0},{4,6},{6,4},{8,10},{10,8},{12,14},{14,12},{1,3},{3,1},... | collective-permute-start | bytes 393224 | tf_op jit(solution)/shard_map/ppermute | solution.py:567
  72.2 1.7 %collective-permute-start.14 = (bf16[256,256]{1,0:T(8,128)(2,1)S(1)}, bf16[256,256]{1,0:T(8,128)(2,1)S(1)}, u32[]{:S(2)}, u32[]{:S(2)}) collective-permute-start(bf16[256,256]{1,0:T(8,128)(2,1)S(1)} %get-tuple-element.46), channel_id=1, source_target_pairs={{0,4},{2,6},{4,0},{6,2},{8,12},{10,14},{12,8},{14,10},{1,5},{3,7},... | collective-permute-start | bytes 393224 | tf_op jit(solution)/shard_map/ppermute | solution.py:567
  74.9 2.1 %collective-permute-start.19 = (bf16[128,256]{1,0:T(8,128)(2,1)S(1)}, bf16[128,256]{1,0:T(8,128)(2,1)S(1)}, u32[]{:S(2)}, u32[]{:S(2)}) collective-permute-start(bf16[128,256]{1,0:T(8,128)(2,1)S(1)} %get-tuple-element.53), channel_id=1, source_target_pairs={{0,6},{2,4},{4,2},{6,0},{8,14},{10,12},{12,10},{14,8},{1,7},{3,5},... | collective-permute-start | bytes 196616 | tf_op jit(solution)/shard_map/ppermute | solution.py:567
  78.5 1.9 %collective-permute-start.21 = (bf16[128,256]{1,0:T(8,128)(2,1)S(1)}, bf16[128,256]{1,0:T(8,128)(2,1)S(1)}, u32[]{:S(2)}, u32[]{:S(2)}) collective-permute-start(bf16[128,256]{1,0:T(8,128)(2,1)S(1)} %get-tuple-element.49), channel_id=1, source_target_pairs={{0,8},{2,10},{4,12},{6,14},{8,0},{10,2},{12,4},{14,6},{1,9},{3,11}... | collective-permute-start | bytes 196616 | tf_op jit(solution)/shard_map/ppermute | solution.py:567
  81.5 1.4 %collective-permute-start.22 = (bf16[128,256]{1,0:T(8,128)(2,1)S(1)}, bf16[128,256]{1,0:T(8,128)(2,1)S(1)}, u32[]{:S(2)}, u32[]{:S(2)}) collective-permute-start(bf16[128,256]{1,0:T(8,128)(2,1)S(1)} %get-tuple-element.50), channel_id=1, source_target_pairs={{0,10},{2,8},{4,14},{6,12},{8,2},{10,0},{12,6},{14,4},{1,11},{3,9}... | collective-permute-start | bytes 196616 | tf_op jit(solution)/shard_map/ppermute | solution.py:567
  83.5 3.4 %collective-permute-start.23 = (bf16[128,256]{1,0:T(8,128)(2,1)S(1)}, bf16[128,256]{1,0:T(8,128)(2,1)S(1)}, u32[]{:S(2)}, u32[]{:S(2)}) collective-permute-start(bf16[128,256]{1,0:T(8,128)(2,1)S(1)} %get-tuple-element.51), channel_id=1, source_target_pairs={{0,12},{2,14},{4,8},{6,10},{8,4},{10,6},{12,0},{14,2},{1,13},{3,15... | collective-permute-start | bytes 196616 | tf_op jit(solution)/shard_map/ppermute | solution.py:567
  86.9 2.1 %collective-permute-start.24 = (bf16[128,256]{1,0:T(8,128)(2,1)S(1)}, bf16[128,256]{1,0:T(8,128)(2,1)S(1)}, u32[]{:S(2)}, u32[]{:S(2)}) collective-permute-start(bf16[128,256]{1,0:T(8,128)(2,1)S(1)} %get-tuple-element.52), channel_id=1, source_target_pairs={{0,14},{2,12},{4,10},{6,8},{8,6},{10,4},{12,2},{14,0},{1,15},{3,13... | collective-permute-start | bytes 196616 | tf_op jit(solution)/shard_map/ppermute | solution.py:567
  89.8 4.1 %collective-permute-done.24.refs_3_ = bf16[128,256]{1,0:T(8,128)(2,1)S(1)} collective-permute-done((bf16[128,256]{1,0:T(8,128)(2,1)S(1)}, bf16[128,256]{1,0:T(8,128)(2,1)S(1)}, u32[]{:S(2)}, u32[]{:S(2)}) %collective-permute-start.24) | collective-permute-done | bytes 65568 | tf_op jit(solution)/shard_map/ppermute | solution.py:567
  93.9 4.8 %convolve.1 = bf16[2048,256]{1,0:T(8,128)(2,1)} custom-call(s32[2]{0:T(128)S(1)} %pad_add_fusion.place, bf16[64,256]{1,0:T(8,128)(2,1)S(1)} %collective-permute-done.20.top.bottom, bf16[64,256]{1,0:T(8,128)(2,1)S(1)} %collective-permute-done.20.top.bottom, bf16[128,256]{1,0:T(8,128)(2,1)S(1)} %collective-permute-done.21.refs_0_, ...), custom_call_target="tpu_custom_call" | custom-call | flops 2415919104 | bytes 2097152 | tf_op jit(solution)/shard_map/convolve/pallas_call | solution.py:510
  (58 shorter events, 15.9 us)
Async XLA Ops:
  0.0 16.2 %collective-permute-start.6 = (bf16[512,256]{1,0:T(8,128)(2,1)}, bf16[512,256]{1,0:T(8,128)(2,1)S(1)}, u32[]{:S(2)}, u32[]{:S(2)}) collective-permute-start(bf16[512,256]{1,0:T(8,128)(2,1)} %bitcast.17), channel_id=1, source_target_pairs={{0,8},{2,10},{4,12},{6,14},{8,0},{10,2},{12,4},{14,6},{1,9},{3,11}... | collective-permute-start | bytes 786440 | tf_op jit(solution)/shard_map/ppermute | solution.py:567
  4.1 14.1 %collective-permute-start = (bf16[512,256]{1,0:T(8,128)(2,1)}, bf16[512,256]{1,0:T(8,128)(2,1)S(1)}, u32[]{:S(2)}, u32[]{:S(2)}) collective-permute-start(bf16[512,256]{1,0:T(8,128)(2,1)} %bitcast.18), channel_id=1, source_target_pairs={{0,1},{1,0},{2,3},{3,2},{4,5},{5,4},{6,7},{7,6},{8,9},{9,8},{10,11... | collective-permute-start | bytes 786440 | tf_op jit(solution)/shard_map/ppermute | solution.py:561
  16.2 24.7 %collective-permute-start.7 = (bf16[512,256]{1,0:T(8,128)(2,1)S(1)}, bf16[512,256]{1,0:T(8,128)(2,1)S(1)}, u32[]{:S(2)}, u32[]{:S(2)}) collective-permute-start(bf16[512,256]{1,0:T(8,128)(2,1)S(1)} %collective-permute-done.6.refs_0_), channel_id=1, source_target_pairs={{0,1},{1,0},{2,3},{3,2},{4,5},{5,4},{6,7},{7,6},{8,9},{9,8},{10,11... | collective-permute-start | bytes 786440 | tf_op jit(solution)/shard_map/ppermute | solution.py:561
  16.2 1.6 %collective-permute-start.1 = (f32[16,512]{1,0:T(8,128)}, f32[16,512]{1,0:T(8,128)S(1)}, u32[]{:S(2)}, u32[]{:S(2)}) collective-permute-start(f32[16,512]{1,0:T(8,128)} %bitcast.20), channel_id=1, source_target_pairs={{0,1},{1,0},{2,3},{3,2},{4,5},{5,4},{6,7},{7,6},{8,9},{9,8},{10,11... | collective-permute-start | bytes 98312 | tf_op jit(solution)/shard_map/ppermute | solution.py:561
  16.7 1.4 %collective-permute-start.2 = (s32[16,512]{1,0:T(8,128)}, s32[16,512]{1,0:T(8,128)S(1)}, u32[]{:S(2)}, u32[]{:S(2)}) collective-permute-start(s32[16,512]{1,0:T(8,128)} %bitcast.14), channel_id=1, source_target_pairs={{0,1},{1,0},{2,3},{3,2},{4,5},{5,4},{6,7},{7,6},{8,9},{9,8},{10,11... | collective-permute-start | bytes 98312 | tf_op jit(solution)/shard_map/ppermute | solution.py:561
  26.3 18.0 %collective-permute-start.3 = (bf16[256,256]{1,0:T(8,128)(2,1)S(1)}, bf16[256,256]{1,0:T(8,128)(2,1)S(1)}, u32[]{:S(2)}, u32[]{:S(2)}) collective-permute-start(bf16[256,256]{1,0:T(8,128)(2,1)S(1)} %get-tuple-element.30), channel_id=1, source_target_pairs={{0,2},{2,0},{4,6},{6,4},{8,10},{10,8},{12,14},{14,12},{1,3},{3,1},... | collective-permute-start | bytes 393224 | tf_op jit(solution)/shard_map/ppermute | solution.py:567
  27.9 4.9 %collective-permute-start.8 = (f32[16,512]{1,0:T(8,128)S(1)}, f32[16,512]{1,0:T(8,128)S(1)}, u32[]{:S(2)}, u32[]{:S(2)}) collective-permute-start(f32[16,512]{1,0:T(8,128)S(1)} %bitcast.22), channel_id=1, source_target_pairs={{0,8},{2,10},{4,12},{6,14},{8,0},{10,2},{12,4},{14,6},{1,9},{3,11}... | collective-permute-start | bytes 98312 | tf_op jit(solution)/shard_map/ppermute | solution.py:567
  38.9 8.3 %collective-permute-start.4 = (bf16[256,256]{1,0:T(8,128)(2,1)S(1)}, bf16[256,256]{1,0:T(8,128)(2,1)S(1)}, u32[]{:S(2)}, u32[]{:S(2)}) collective-permute-start(bf16[256,256]{1,0:T(8,128)(2,1)S(1)} %get-tuple-element.31), channel_id=1, source_target_pairs={{0,4},{2,6},{4,0},{6,2},{8,12},{10,14},{12,8},{14,10},{1,5},{3,7},... | collective-permute-start | bytes 393224 | tf_op jit(solution)/shard_map/ppermute | solution.py:567
  40.0 8.1 %collective-permute-start.5 = (bf16[256,256]{1,0:T(8,128)(2,1)S(1)}, bf16[256,256]{1,0:T(8,128)(2,1)S(1)}, u32[]{:S(2)}, u32[]{:S(2)}) collective-permute-start(bf16[256,256]{1,0:T(8,128)(2,1)S(1)} %get-tuple-element.32), channel_id=1, source_target_pairs={{0,6},{2,4},{4,2},{6,0},{8,14},{10,12},{12,10},{14,8},{1,7},{3,5},... | collective-permute-start | bytes 393224 | tf_op jit(solution)/shard_map/ppermute | solution.py:567
  41.7 7.8 %collective-permute-start.10 = (bf16[256,256]{1,0:T(8,128)(2,1)S(1)}, bf16[256,256]{1,0:T(8,128)(2,1)S(1)}, u32[]{:S(2)}, u32[]{:S(2)}) collective-permute-start(bf16[256,256]{1,0:T(8,128)(2,1)S(1)} %get-tuple-element.34), channel_id=1, source_target_pairs={{0,2},{2,0},{4,6},{6,4},{8,10},{10,8},{12,14},{14,12},{1,3},{3,1},... | collective-permute-start | bytes 393224 | tf_op jit(solution)/shard_map/ppermute | solution.py:567
  43.3 7.7 %collective-permute-start.11 = (bf16[256,256]{1,0:T(8,128)(2,1)S(1)}, bf16[256,256]{1,0:T(8,128)(2,1)S(1)}, u32[]{:S(2)}, u32[]{:S(2)}) collective-permute-start(bf16[256,256]{1,0:T(8,128)(2,1)S(1)} %get-tuple-element.35), channel_id=1, source_target_pairs={{0,4},{2,6},{4,0},{6,2},{8,12},{10,14},{12,8},{14,10},{1,5},{3,7},... | collective-permute-start | bytes 393224 | tf_op jit(solution)/shard_map/ppermute | solution.py:567
  44.4 8.6 %collective-permute-start.12 = (bf16[256,256]{1,0:T(8,128)(2,1)S(1)}, bf16[256,256]{1,0:T(8,128)(2,1)S(1)}, u32[]{:S(2)}, u32[]{:S(2)}) collective-permute-start(bf16[256,256]{1,0:T(8,128)(2,1)S(1)} %get-tuple-element.36), channel_id=1, source_target_pairs={{0,6},{2,4},{4,2},{6,0},{8,14},{10,12},{12,10},{14,8},{1,7},{3,5},... | collective-permute-start | bytes 393224 | tf_op jit(solution)/shard_map/ppermute | solution.py:567
  60.7 14.2 %collective-permute-start.16 = (bf16[4,128,256]{2,1,0:T(8,128)(2,1)S(1)}, bf16[4,128,256]{2,1,0:T(8,128)(2,1)S(1)}, u32[]{:S(2)}, u32[]{:S(2)}) collective-permute-start(bf16[4,128,256]{2,1,0:T(8,128)(2,1)S(1)} %get-tuple-element.48), channel_id=1, source_target_pairs={{0,8},{2,10},{4,12},{6,14},{8,0},{10,2},{12,4},{14,6},{1,9},{3,11}... | collective-permute-start | bytes 786440 | tf_op jit(solution)/shard_map/ppermute | solution.py:567
  70.6 7.3 %collective-permute-start.13 = (bf16[256,256]{1,0:T(8,128)(2,1)S(1)}, bf16[256,256]{1,0:T(8,128)(2,1)S(1)}, u32[]{:S(2)}, u32[]{:S(2)}) collective-permute-start(bf16[256,256]{1,0:T(8,128)(2,1)S(1)} %get-tuple-element.45), channel_id=1, source_target_pairs={{0,2},{2,0},{4,6},{6,4},{8,10},{10,8},{12,14},{14,12},{1,3},{3,1},... | collective-permute-start | bytes 393224 | tf_op jit(solution)/shard_map/ppermute | solution.py:567
  72.2 6.4 %collective-permute-start.14 = (bf16[256,256]{1,0:T(8,128)(2,1)S(1)}, bf16[256,256]{1,0:T(8,128)(2,1)S(1)}, u32[]{:S(2)}, u32[]{:S(2)}) collective-permute-start(bf16[256,256]{1,0:T(8,128)(2,1)S(1)} %get-tuple-element.46), channel_id=1, source_target_pairs={{0,4},{2,6},{4,0},{6,2},{8,12},{10,14},{12,8},{14,10},{1,5},{3,7},... | collective-permute-start | bytes 393224 | tf_op jit(solution)/shard_map/ppermute | solution.py:567
  73.9 7.6 %collective-permute-start.15 = (bf16[256,256]{1,0:T(8,128)(2,1)S(1)}, bf16[256,256]{1,0:T(8,128)(2,1)S(1)}, u32[]{:S(2)}, u32[]{:S(2)}) collective-permute-start(bf16[256,256]{1,0:T(8,128)(2,1)S(1)} %get-tuple-element.47), channel_id=1, source_target_pairs={{0,6},{2,4},{4,2},{6,0},{8,14},{10,12},{12,10},{14,8},{1,7},{3,5},... | collective-permute-start | bytes 393224 | tf_op jit(solution)/shard_map/ppermute | solution.py:567
  74.9 8.7 %collective-permute-start.19 = (bf16[128,256]{1,0:T(8,128)(2,1)S(1)}, bf16[128,256]{1,0:T(8,128)(2,1)S(1)}, u32[]{:S(2)}, u32[]{:S(2)}) collective-permute-start(bf16[128,256]{1,0:T(8,128)(2,1)S(1)} %get-tuple-element.53), channel_id=1, source_target_pairs={{0,6},{2,4},{4,2},{6,0},{8,14},{10,12},{12,10},{14,8},{1,7},{3,5},... | collective-permute-start | bytes 196616 | tf_op jit(solution)/shard_map/ppermute | solution.py:567
  76.9 10.0 %collective-permute-start.18 = (bf16[128,256]{1,0:T(8,128)(2,1)S(1)}, bf16[128,256]{1,0:T(8,128)(2,1)S(1)}, u32[]{:S(2)}, u32[]{:S(2)}) collective-permute-start(bf16[128,256]{1,0:T(8,128)(2,1)S(1)} %get-tuple-element.54), channel_id=1, source_target_pairs={{0,4},{2,6},{4,0},{6,2},{8,12},{10,14},{12,8},{14,10},{1,5},{3,7},... | collective-permute-start | bytes 196616 | tf_op jit(solution)/shard_map/ppermute | solution.py:567
  77.9 11.2 %collective-permute-start.17 = (bf16[128,256]{1,0:T(8,128)(2,1)S(1)}, bf16[128,256]{1,0:T(8,128)(2,1)S(1)}, u32[]{:S(2)}, u32[]{:S(2)}) collective-permute-start(bf16[128,256]{1,0:T(8,128)(2,1)S(1)} %get-tuple-element.55), channel_id=1, source_target_pairs={{0,2},{2,0},{4,6},{6,4},{8,10},{10,8},{12,14},{14,12},{1,3},{3,1},... | collective-permute-start | bytes 196616 | tf_op jit(solution)/shard_map/ppermute | solution.py:567
  78.5 11.2 %collective-permute-start.21 = (bf16[128,256]{1,0:T(8,128)(2,1)S(1)}, bf16[128,256]{1,0:T(8,128)(2,1)S(1)}, u32[]{:S(2)}, u32[]{:S(2)}) collective-permute-start(bf16[128,256]{1,0:T(8,128)(2,1)S(1)} %get-tuple-element.49), channel_id=1, source_target_pairs={{0,8},{2,10},{4,12},{6,14},{8,0},{10,2},{12,4},{14,6},{1,9},{3,11}... | collective-permute-start | bytes 196616 | tf_op jit(solution)/shard_map/ppermute | solution.py:567
  81.5 8.3 %collective-permute-start.22 = (bf16[128,256]{1,0:T(8,128)(2,1)S(1)}, bf16[128,256]{1,0:T(8,128)(2,1)S(1)}, u32[]{:S(2)}, u32[]{:S(2)}) collective-permute-start(bf16[128,256]{1,0:T(8,128)(2,1)S(1)} %get-tuple-element.50), channel_id=1, source_target_pairs={{0,10},{2,8},{4,14},{6,12},{8,2},{10,0},{12,6},{14,4},{1,11},{3,9}... | collective-permute-start | bytes 196616 | tf_op jit(solution)/shard_map/ppermute | solution.py:567
  83.5 6.3 %collective-permute-start.23 = (bf16[128,256]{1,0:T(8,128)(2,1)S(1)}, bf16[128,256]{1,0:T(8,128)(2,1)S(1)}, u32[]{:S(2)}, u32[]{:S(2)}) collective-permute-start(bf16[128,256]{1,0:T(8,128)(2,1)S(1)} %get-tuple-element.51), channel_id=1, source_target_pairs={{0,12},{2,14},{4,8},{6,10},{8,4},{10,6},{12,0},{14,2},{1,13},{3,15... | collective-permute-start | bytes 196616 | tf_op jit(solution)/shard_map/ppermute | solution.py:567
  86.9 7.0 %collective-permute-start.24 = (bf16[128,256]{1,0:T(8,128)(2,1)S(1)}, bf16[128,256]{1,0:T(8,128)(2,1)S(1)}, u32[]{:S(2)}, u32[]{:S(2)}) collective-permute-start(bf16[128,256]{1,0:T(8,128)(2,1)S(1)} %get-tuple-element.52), channel_id=1, source_target_pairs={{0,14},{2,12},{4,10},{6,8},{8,6},{10,4},{12,2},{14,0},{1,15},{3,13... | collective-permute-start | bytes 196616 | tf_op jit(solution)/shard_map/ppermute | solution.py:567
  89.7 4.2 %collective-permute-start.20 = (bf16[64,256]{1,0:T(8,128)(2,1)S(1)}, bf16[64,256]{1,0:T(8,128)(2,1)S(1)}, u32[]{:S(2)}, u32[]{:S(2)}) collective-permute-start(bf16[64,256]{1,0:T(8,128)(2,1)S(1)} %edges.1), channel_id=1, source_target_pairs={{0,1},{1,0},{2,3},{3,2},{4,5},{5,4},{6,7},{7,6},{8,9},{9,8},{10,11... | collective-permute-start | bytes 98312 | tf_op jit(solution)/shard_map/ppermute | solution.py:612
  (12 other events, 161.0 us)
where the time goes:
time: 99 us; the launch traced here: 98.7 us
  Pallas kernels  33.1 us (33%)
  waiting for transfers between devices  32 us (32%)
  starting transfers between devices  30 us (30%)
  local copies, waits for them, and re-layouts  3.28 us (3%)
    ppermute x19, starting transfers between devices, swap(): return lax.ppermute(value, 'tm', [(i, i ^ k) for i in range(slots)])  29.5 us
    ppermute x19, waiting for transfers between devices, swap(): return lax.ppermute(value, 'tm', [(i, i ^ k) for i in range(slots)])  29.4 us
    pallas_call x2, Pallas kernels, encode(): pl.pallas_call(functools.partial(encode_kernel, slots=slots, chunk=chunk,...  15.4 us
    pallas_call x1, Pallas kernels, pool(): pl.pallas_call(functools.partial(pool_kernel, slots=slots, piece_rows=pie...  5.65 us
    pallas_call x1, Pallas kernels, convolve(): pl.pallas_call(functools.partial(conv_kernel, layout=layout, chunks=chunk...  4.77 us
    pallas_call x1, Pallas kernels, pool_matrix(): pl.pallas_call(functools.partial(match_kernel, slots=slots, piece_rows=pi...  4.07 us
    unnamed x22, local copies, waits for them, and re-layouts  3.26 us
    ppermute x5, waiting for transfers between devices, from_others(): values.append(lax.ppermute(value, 'sector', ring))  2.55 us
  transfers between devices with their start and end apart: 25, of which 14 were waited for; matrix products, arithmetic and copies ran while one was open for 0% of the time, Pallas kernels for 21%

commit v1 on v0

--- a/solution.py
+++ b/solution.py
@@ -14,6 +14,7 @@
 LANES = 128
 TILE_LANES = 256
 SUBLANES = 8
+MERGED = 2
 VMEM_LIMIT = 24 << 20
 F32 = jnp.float32
 BF16 = jnp.bfloat16
@@ -24,20 +25,42 @@
     bins, pixels = weights[0].shape
     wide = (SUBLANES, pixels)
     column = lax.broadcasted_iota(jnp.int32, wide, 0).astype(F32).astype(BF16)
+    tiles = [slice(low, low + SUBLANES) for low in range(0, GRID, SUBLANES)]
+    count = math.gcd(bins, MERGED)
+
+    def spread(line):
+        return jnp.broadcast_to(line, wide).astype(BF16)
+
     for s in range(len(weights)):
-        rows = lax.div(ids[s][...], GRID)
-        cols = (ids[s][...] - rows * GRID).astype(F32)
-        rows = rows.astype(F32)
-        for d in range(bins):
-            row_id[s, d] = jnp.broadcast_to(rows[d : d + 1], wide).astype(BF16)
-            col = jnp.broadcast_to(cols[d : d + 1], wide).astype(BF16)
-            value = jnp.broadcast_to(weights[s][d : d + 1, :], wide).astype(BF16)
-            for j in range(GRID // SUBLANES):
-                low = j * SUBLANES
-                hit = column + low == col
-                col_hot[s, d, low : low + SUBLANES] = jnp.where(
-                    hit, value, jnp.zeros_like(value)
-                )
+
+        def merge(n, _):
+            row, hot = [], []
+            for k in range(count):
+                d = n * count + k
+                cell = ids[s][pl.ds(d, 1), :]
+                line = cell >> (GRID.bit_length() - 1)
+                row.append(spread(line.astype(F32)))
+                col = spread((cell & (GRID - 1)).astype(F32))
+                value = spread(weights[s][pl.ds(d, 1), :])
+                hot.append((col, value))
+            for at in tiles:
+                parts = []
+                for col, value in hot:
+                    hit = column + at.start == col
+                    parts.append(jnp.where(hit, value, jnp.zeros_like(value)))
+                for k in range(count):
+                    for later in range(k + 1, count):
+                        more = jnp.where(row[later] == row[k], parts[later], jnp.zeros(wide, BF16))
+                        parts[k] = parts[k] + more
+                    col_hot[s, n * count + k, at] = parts[k]
+            for k in range(count):
+                lone = row[k]
+                for earlier in range(k):
+                    lone = jnp.where(row[earlier] == row[k], jnp.full(wide, -1.0, BF16), lone)
+                row_id[s, n * count + k] = lone
+            return 0
+
+        lax.fori_loop(0, bins // count, merge, 0)
 
 
 def match(place, slot, matrix, base, col_hot, row_id, piece_rows, chunk_order):
@@ -55,13 +78,18 @@
             s = n // blocks
             at = pl.ds(pl.multiple_of((n % blocks) * TILE_LANES, TILE_LANES), TILE_LANES)
             sums = [[jnp.zeros(shape, BF16)] * (GRID // SUBLANES) for _ in targets]
-            for d in range(bins):
-                row = row_id[s, d, :, at]
-                hits = [row == target for target in targets]
+            count = math.gcd(bins, MERGED)
+            for low in range(0, bins, count):
+                group = range(low, low + count)
+                hits = [[row_id[s, d, :, at] == target for target in targets] for d in group]
                 for j in range(GRID // SUBLANES):
-                    part = col_hot[s, d, j * SUBLANES : (j + 1) * SUBLANES, at]
-                    for k, hit in enumerate(hits):
-                        sums[k][j] = sums[k][j] + jnp.where(hit, part, jnp.zeros_like(part))
+                    tile = slice(j * SUBLANES, (j + 1) * SUBLANES)
+                    found = [jnp.zeros(shape, BF16) for _ in targets]
+                    for d, hit in zip(group, hits):
+                        part = col_hot[s, d, tile, at]
+                        found = [jnp.where(h, part, f) for h, f in zip(hit, found)]
+                    for k in range(len(targets)):
+                        sums[k][j] = sums[k][j] + found[k]
             for k in range(len(targets)):
                 for j in range(GRID // SUBLANES):
                     low = base + (first + k) * GRID + j * SUBLANES
@@ -107,14 +135,17 @@
         match(place, slot, matrix, n * cells, col_hot, row_id, piece_rows, chunk_order)
 
 
-def multiply_kernel(*refs, sectors):
+def multiply_kernel(*refs, sectors, chunks):
     contexts, matrix = refs[:sectors], refs[sectors]
     out_refs, context_t = refs[sectors + 1 : -1], refs[-1]
     for s in range(sectors):
         context_t[s] = contexts[s][...].astype(F32).T.astype(BF16)
-    cells = matrix.shape[1] // len(out_refs)
-    for n, out_ref in enumerate(out_refs):
-        out_ref[...] = multiply(context_t, matrix, n * cells, cells)
+    valid = matrix.shape[1] // len(out_refs)
+    cells = valid * chunks
+    for n in range(len(out_refs) // chunks):
+        done = multiply(context_t, matrix, n * cells, cells)
+        for c in range(chunks):
+            out_refs[n * chunks + c][...] = done[:, c * valid : (c + 1) * valid]
 
 
 def hot_scratch(sectors, bins, pixels):
@@ -177,15 +208,16 @@
     )(place, *[a for args in zip(depths, ids) for a in args])
 
 
-def pool_multiply(contexts, matrix, count):
+def pool_multiply(contexts, matrix, slots, chunks):
     pixels, channels = contexts[0].shape
-    cells = matrix.shape[1] // count
+    cells = matrix.shape[1] // slots
+    valid = cells // chunks
     vmem = pl.BlockSpec(memory_space=pltpu.VMEM)
-    return pl.pallas_call(
-        functools.partial(multiply_kernel, sectors=len(contexts)),
-        out_shape=[jax.ShapeDtypeStruct((channels, cells), BF16)] * count,
+    outs = pl.pallas_call(
+        functools.partial(multiply_kernel, sectors=len(contexts), chunks=chunks),
+        out_shape=[jax.ShapeDtypeStruct((channels, valid), BF16)] * (slots * chunks),
         in_specs=[vmem] * (len(contexts) + 1),
-        out_specs=[vmem] * count,
+        out_specs=[vmem] * (slots * chunks),
         scratch_shapes=[pltpu.VMEM((len(contexts), channels, pixels), BF16)],
         compiler_params=pltpu.CompilerParams(vmem_limit_bytes=VMEM_LIMIT),
         cost_estimate=pl.CostEstimate(
@@ -195,6 +227,7 @@
         ),
         name="pool_multiply",
     )(*contexts, matrix)
+    return [outs[n * chunks : (n + 1) * chunks] for n in range(slots)]
 
 
 def prep_kernel(w_qkv, w_out, w_up, w_down, gain, embed, qkv_t, out_t, up_t, down_t, gains, embeds):
@@ -342,7 +375,7 @@
         frame = place[0] ^ k
         for lane in range(0, cells, LANES):
             at = pl.ds(pl.multiple_of(frame * cells + lane, LANES), LANES)
-            low = chunk * cells + lane
+            low = lane + (chunk * cells if tokens[k].shape[1] > cells else 0)
             stream[:, at] = tokens[k][:, low : low + LANES].astype(F32) + embed[frame]
 
     def layer(l, _):
@@ -374,7 +407,7 @@
     earlier, outs = outs[:chunk] if last else [], outs[chunk:] if last else outs
     for k in range(slots):
         at = pl.ds(pl.multiple_of((place[0] ^ k) * cells, LANES), cells)
-        done = stream[:, at].T.astype(BF16)[:valid]
+        done = stream[:, at].astype(BF16).T[:valid]
         if not last:
             outs[k // half][k % half] = done
         elif k >= half:
@@ -388,8 +421,7 @@
 def encode(place, tokens, weights, gains, embed, earlier, chunk, chunks):
     slots = len(tokens)
     half = slots // 2
-    channels, piece_cells = tokens[0].shape
-    valid = piece_cells // chunks
+    channels, valid = tokens[-1].shape
     spare = -valid % LANES
     if spare:
         tokens = [jnp.pad(t, ((0, 0), (0, spare))) for t in tokens]
@@ -463,9 +495,13 @@
     )(place, *parts)
 
 
-def conv_kernel(place, top, bottom, *refs, layout, chunks, piece_rows, bands, block):
-    *parts, weight, out_ref, rows = refs
+def conv_kernel(place, top, bottom, *refs, layout, chunks, piece_rows, bands, block, part):
+    *refs, out_ref, rows, outs, sent = refs
+    if part == "rest":
+        refs = refs[:-1]
+    *parts, weight = refs
     slots = len(layout)
+    half = slots // 2
     total = slots * piece_rows
     inside = (place[1] > 0, place[1] < (bands - 1) * total)
     for edge, has, low in ((top, inside[0], 0), (bottom, inside[1], (total + 1) * GRID)):
@@ -474,6 +510,8 @@
     for k in range(slots):
         base = (1 + (place[0] ^ k) * piece_rows) * GRID
         for c, chunk in enumerate(chunks):
+            if layout[k][c] is None:
+                continue
             source, start = layout[k][c]
             for i, row in enumerate(chunk):
                 low = pl.multiple_of(base + row * GRID, GRID)
@@ -482,31 +520,63 @@
 
     cells = block * GRID
     column = lax.broadcasted_iota(jnp.int32, (cells, 1), 0) % GRID
+    own = place[0] // half
+    each = total // block // 2
+    blocks = {"all": 2 * each, "inner": each - 2, "rest": each + 2}[part]
+
+    def block_at(n):
+        if part == "all":
+            return n
+        if part == "inner":
+            return own * each + 1 + n
+        end = own * each + jnp.where(n == each, 0, each - 1)
+        return jnp.where(n < each, (1 - own) * each + n, end)
+
+    def send(n):
+        at = pl.ds(pl.multiple_of(block_at(n) * cells, cells), cells)
+        here = pl.ds(pl.multiple_of(n * cells, cells), cells)
+        return pltpu.make_async_copy(outs.at[here], out_ref.at[at], sent.at[n])
 
     def one_block(n, _):
+        where = block_at(n)
+
         def taps(j):
             sums = None
             for i in range(3):
-                at = pl.ds(pl.multiple_of((n * block + i) * GRID, GRID), cells)
+                at = pl.ds(pl.multiple_of((where * block + i) * GRID, GRID), cells)
                 product = jnp.dot(rows[at], weight[i, j], preferred_element_type=F32)
                 sums = product if sums is None else sums + product
             return sums
 
-        at = pl.ds(pl.multiple_of((n * block + 1) * GRID, GRID), cells)
+        at = pl.ds(pl.multiple_of((where * block + 1) * GRID, GRID), cells)
         summed = rows[at].astype(F32) + taps(1)
         summed = summed + jnp.where(column == 0, 0.0, pltpu.roll(taps(0), 1, 0))
         summed = summed + jnp.where(column == GRID - 1, 0.0, pltpu.roll(taps(2), cells - 1, 0))
-        out_ref[pl.ds(pl.multiple_of(n * cells, cells), cells)] = summed.astype(BF16)
+        outs[pl.ds(pl.multiple_of(n * cells, cells), cells)] = summed.astype(BF16)
+        send(n).start()
         return 0
 
-    lax.fori_loop(0, total // block, one_block, 0)
-
-
-def convolve(place, top, bottom, parts, weight, layout, chunks, bands):
+    lax.fori_loop(0, blocks, one_block, 0)
+    for n in range(blocks):
+        send(n).wait()
+
+
+def convolve(place, top, bottom, parts, weight, layout, chunks, bands, part, before=None):
     channels = weight.shape[-1]
     piece_rows = sum(len(chunk) for chunk in chunks)
     total = len(layout) * piece_rows
+    block = math.gcd(total // 2, 4)
+    each = total // block // 2
+    done = {"all": 2 * each, "inner": each - 2, "rest": each + 2}[part] * block
     vmem = pl.BlockSpec(memory_space=pltpu.VMEM)
+    hbm = pl.BlockSpec(memory_space=pltpu.HBM)
+    operands = [place, top, bottom, *parts, weight]
+    aliases = {}
+    in_specs = [pl.BlockSpec(memory_space=pltpu.SMEM)] + [vmem] * (len(operands) - 1)
+    if part == "rest":
+        aliases = {len(operands): 0}
+        operands.append(before)
+        in_specs.append(hbm)
     return pl.pallas_call(
         functools.partial(
             conv_kernel,
@@ -514,20 +584,26 @@
             chunks=chunks,
             piece_rows=piece_rows,
             bands=bands,
-            block=math.gcd(total, 8),
+            block=block,
+            part=part,
         ),
         out_shape=jax.ShapeDtypeStruct((total * GRID, channels), BF16),
-        in_specs=[pl.BlockSpec(memory_space=pltpu.SMEM)] + [vmem] * (len(parts) + 3),
-        out_specs=vmem,
-        scratch_shapes=[pltpu.VMEM(((total + 2) * GRID, channels), BF16)],
+        in_specs=in_specs,
+        out_specs=hbm,
+        scratch_shapes=[
+            pltpu.VMEM(((total + 2) * GRID, channels), BF16),
+            pltpu.VMEM((done * GRID, channels), BF16),
+            pltpu.SemaphoreType.DMA((done // block,)),
+        ],
+        input_output_aliases=aliases,
         compiler_params=pltpu.CompilerParams(vmem_limit_bytes=VMEM_LIMIT),
         cost_estimate=pl.CostEstimate(
-            flops=2 * total * GRID * weight.size,
-            bytes_accessed=4 * total * GRID * channels,
+            flops=2 * done * GRID * weight.size,
+            bytes_accessed=4 * done * GRID * channels,
             transcendentals=0,
         ),
         name="convolve",
-    )(place, top, bottom, *parts, weight)
+    )(*operands)
 
 
 def row_chunks(piece_rows):
@@ -578,42 +654,53 @@
     tokens = [swap(own[k], k) for k in near]
     matrix = pool_matrix(place, depths_partner, ids, near, *order)
     contexts = from_others(features)
-    partner = pool_multiply(contexts, matrix, half)
-    tokens += [swap(partner[k], k) for k in near]
+    partner = pool_multiply(contexts, matrix, half, len(chunks))
+    later_tokens = [[swap(partner[k][c], k) for k in near] for c in range(len(chunks))]
     *weights, gains, embed = prep(w_qkv, w_out, w_up, w_down, norm_gain, time_embed)
 
     earlier, crossed = [], []
     for c in range(len(chunks) - 1):
-        near_part, far_part = encode(place, tokens, weights, gains, embed, [], c, len(chunks))
+        slot_tokens = tokens + later_tokens[c]
+        near_part, far_part = encode(
+            place, slot_tokens, weights, gains, embed, [], c, len(chunks)
+        )
         earlier.append(near_part)
         crossed.append(swap(far_part, half))
+    slot_tokens = tokens + later_tokens[-1]
     outs = encode(
-        place, tokens, weights, gains, embed, earlier, len(chunks) - 1, len(chunks)
+        place, slot_tokens, weights, gains, embed, earlier, len(chunks) - 1, len(chunks)
     )
     parts, layout = [], [[None] * len(chunks) for _ in range(slots)]
-
-    for k in range(half, slots):
-        parts.append(swap(outs[k], k))
-        layout[k][-1] = (len(parts) - 1, 0)
     for k in near:
         parts.append(swap(outs[k], k))
         for c in range(len(chunks)):
             layout[k][c] = (len(parts) - 1, c * valid)
+    early_parts, early_layout = list(parts), [list(places) for places in layout]
     for c, received in enumerate(crossed):
         for k in near:
             parts.append(swap(received[k], k))
             layout[half + k][c] = (len(parts) - 1, 0)
+    for k in range(half, slots):
+        parts.append(swap(outs[k], k))
+        layout[k][-1] = (len(parts) - 1, 0)
 
     first = [parts[layout[k][0][0]] for k in range(slots)]
     up = [(i, i + 1) for i in range(sectors - 1)]
     down = [(i + 1, i) for i in range(sectors - 1)]
+    ends = edges(place, first, valid, sectors == 2)
     if sectors == 2:
-        (edge,) = edges(place, first, valid, True)
-        top = bottom = lax.ppermute(edge, "sector", up + down)
+        top = bottom = lax.ppermute(ends[0], "sector", up + down)
     else:
-        head, tail = edges(place, first, valid, False)
+        head, tail = ends
         top, bottom = lax.ppermute(tail, "sector", up), lax.ppermute(head, "sector", down)
-    out = convolve(place, top, bottom, parts, conv_weight, layout, chunks, sectors)
+    ends = (conv_weight, layout, chunks, sectors)
+    if len(chunks) > 1:
+        nothing = jnp.zeros_like(top)
+        inner = (conv_weight, early_layout, chunks, sectors)
+        out = convolve(place, nothing, nothing, early_parts, *inner, "inner")
+        out = convolve(place, top, bottom, parts, *ends, "rest", out)
+    else:
+        out = convolve(place, top, bottom, parts, *ends, "all")
     return out.reshape(1, band_rows, GRID, -1)
 
 

time: 99 us -> 93.7 us (0.946)
  waiting for transfers between devices: 32 us -> 22.3 us
  starting transfers between devices: 30 us -> 32.9 us
  Pallas kernels: 33.1 us -> 34.7 us
    ppermute x19 -> x22, waiting for transfers between devices: 29.4 us -> 20.9 us  [swap(): return lax.ppermute(value, 'tm', [(i, i ^ k) for i in range(slots)])]
    ppermute x19 -> x22, starting transfers between devices: 29.5 us -> 32.3 us  [swap(): return lax.ppermute(value, 'tm', [(i, i ^ k) for i in range(slots)])]
    pallas_call x1 -> x2, Pallas kernels: 4.77 us -> 6.51 us  [convolve(): pl.pallas_call(functools.partial(conv_kernel, layout=layout, chunks=chunk...]
    ppermute x5, waiting for transfers between devices: 2.55 us -> 1.35 us  [from_others(): values.append(lax.ppermute(value, 'sector', ring))]
  transfers between devices with their start and end apart: 25 -> 28, of which waited for: 14 -> 7; matrix products, arithmetic and copies ran while one was open for 0% -> 0% of each run, Pallas kernels for 21% -> 33%
where the time goes in v1:
time: 93.7 us; the launch traced here: 93.4 us
  Pallas kernels  34.7 us (37%)
  starting transfers between devices  32.9 us (35%)
  waiting for transfers between devices  22.3 us (24%)
  local copies, waits for them, and re-layouts  3.28 us (4%)
    ppermute x22, starting transfers between devices, swap(): return lax.ppermute(value, 'tm', [(i, i ^ k) for i in range(slots)])  32.3 us
    ppermute x22, waiting for transfers between devices, swap(): return lax.ppermute(value, 'tm', [(i, i ^ k) for i in range(slots)])  20.9 us
    pallas_call x2, Pallas kernels, encode(): pl.pallas_call(functools.partial(encode_kernel, slots=slots, chunk=chunk,...  15.5 us
    pallas_call x2, Pallas kernels, convolve(): pl.pallas_call(functools.partial(conv_kernel, layout=layout, chunks=chunk...  6.51 us
    pallas_call x1, Pallas kernels, pool(): pl.pallas_call(functools.partial(pool_kernel, slots=slots, piece_rows=pie...  5.62 us
    pallas_call x1, Pallas kernels, pool_matrix(): pl.pallas_call(functools.partial(match_kernel, slots=slots, piece_rows=pi...  3.83 us
    unnamed x22, local copies, waits for them, and re-layouts  3.25 us
  transfers between devices with their start and end apart: 28, of which 7 were waited for; matrix products, arithmetic and copies ran while one was open for 0% of the time, Pallas kernels for 33%

profile of v1, /device:TPU:0, one launch (start us, length us, event | category | flops | bytes accessed | tf_op | source)
XLA Modules:
  0.0 93.4 jit_solution(18249669187191482338)
XLA Ops:
  0.0 4.1 %collective-permute-start.6 = (bf16[512,256]{1,0:T(8,128)(2,1)}, bf16[512,256]{1,0:T(8,128)(2,1)S(1)}, u32[]{:S(2)}, u32[]{:S(2)}) collective-permute-start(bf16[512,256]{1,0:T(8,128)(2,1)} %bitcast.17), channel_id=1, source_target_pairs={{0,8},{2,10},{4,12},{6,14},{8,0},{10,2},{12,4},{14,6},{1,9},{3,11}... | collective-permute-start | bytes 786440 | tf_op jit(solution)/shard_map/ppermute | solution.py:643
  4.1 12.1 %collective-permute-done.6.refs_0_ = bf16[512,256]{1,0:T(8,128)(2,1)S(1)} collective-permute-done((bf16[512,256]{1,0:T(8,128)(2,1)}, bf16[512,256]{1,0:T(8,128)(2,1)S(1)}, u32[]{:S(2)}, u32[]{:S(2)}) %collective-permute-start.6) | collective-permute-done | bytes 262176 | tf_op jit(solution)/shard_map/ppermute | solution.py:643
  20.6 5.6 %pool.1 = (bf16[256,256]{1,0:T(8,128)(2,1)S(1)}, bf16[256,256]{1,0:T(8,128)(2,1)S(1)}, bf16[256,256]{1,0:T(8,128)(2,1)S(1)}, bf16[256,256]{1,0:T(8,128)(2,1)S(1)}) custom-call(s32[2]{0:T(128)S(1)} %pad_add_fusion.place, bf16[512,256]{1,0:T(8,128)(2,1)S(1)} %bitcast.19, f32[16,512]{1,0:T(8,128)S(1)} %bitcast.21, s32[16,512]{1,0:T(8,128)S(1)} %bitcast.15, ...), custom_call_target="tpu_custom_call" | custom-call | flops 536870912 | bytes 524288 | tf_op jit(solution)/shard_map/pool/pallas_call | solution.py:164
  26.2 1.6 %collective-permute-start.3 = (bf16[256,256]{1,0:T(8,128)(2,1)S(1)}, bf16[256,256]{1,0:T(8,128)(2,1)S(1)}, u32[]{:S(2)}, u32[]{:S(2)}) collective-permute-start(bf16[256,256]{1,0:T(8,128)(2,1)S(1)} %get-tuple-element.34), channel_id=1, source_target_pairs={{0,2},{2,0},{4,6},{6,4},{8,10},{10,8},{12,14},{14,12},{1,3},{3,1},... | collective-permute-start | bytes 393224 | tf_op jit(solution)/shard_map/ppermute | solution.py:643
  27.9 4.9 %collective-permute-done.8.refs_0_ = f32[16,512]{1,0:T(8,128)S(1)} collective-permute-done((f32[16,512]{1,0:T(8,128)S(1)}, f32[16,512]{1,0:T(8,128)S(1)}, u32[]{:S(2)}, u32[]{:S(2)}) %collective-permute-start.8) | collective-permute-done | bytes 32800 | tf_op jit(solution)/shard_map/ppermute | solution.py:643
  32.8 1.0 %collective-permute-start.4 = (bf16[256,256]{1,0:T(8,128)(2,1)S(1)}, bf16[256,256]{1,0:T(8,128)(2,1)S(1)}, u32[]{:S(2)}, u32[]{:S(2)}) collective-permute-start(bf16[256,256]{1,0:T(8,128)(2,1)S(1)} %get-tuple-element.35), channel_id=1, source_target_pairs={{0,4},{2,6},{4,0},{6,2},{8,12},{10,14},{12,8},{14,10},{1,5},{3,7},... | collective-permute-start | bytes 393224 | tf_op jit(solution)/shard_map/ppermute | solution.py:643
  35.6 3.8 %pool_matrix.1.refs_2_ = bf16[2,1024,512]{2,1,0:T(8,128)(2,1)S(1)} custom-call(s32[2]{0:T(128)S(1)} %pad_add_fusion.place, f32[16,512]{1,0:T(8,128)S(1)} %collective-permute-done.8.refs_0_, s32[16,512]{1,0:T(8,128)S(1)} %bitcast.16, f32[16,512]{1,0:T(8,128)S(1)} %collective-permute-done.9.refs_2_, s32[16,512]{1,0:T(8,128)S(1)} %collective-permute-done.2.refs_5_.refs_3_), custom_call_target="tpu_custom_call" | custom-call | flops 33554432 | bytes 1048576 | tf_op jit(solution)/shard_map/pool_matrix/pallas_call | solution.py:193
  40.2 1.6 %collective-permute-start.13 = (bf16[256,128]{1,0:T(8,128)(2,1)S(1)}, bf16[256,128]{1,0:T(8,128)(2,1)S(1)}, u32[]{:S(2)}, u32[]{:S(2)}) collective-permute-start(bf16[256,128]{1,0:T(8,128)(2,1)S(1)} %get-tuple-element.48), channel_id=1, source_target_pairs={{0,2},{2,0},{4,6},{6,4},{8,10},{10,8},{12,14},{14,12},{1,3},{3,1},... | collective-permute-start | bytes 196616 | tf_op jit(solution)/shard_map/ppermute | solution.py:643
  43.8 1.8 %prep.1 = (bf16[2,768,256]{2,1,0:T(8,128)(2,1)S(1)}, bf16[2,256,256]{2,1,0:T(8,128)(2,1)S(1)}, bf16[2,1024,256]{2,1,0:T(8,128)(2,1)S(1)}, bf16[2,256,1024]{2,1,0...) custom-call(bf16[2,256,768]{2,1,0:T(8,128)(2,1)S(1)} %copy-done.3, ...), custom_call_target="tpu_custom_call" | custom-call | flops 805306368 | bytes 6291456 | tf_op jit(solution)/shard_map/prep/pallas_call | solution.py:274
  45.7 1.6 %collective-permute-start.10 = (bf16[256,128]{1,0:T(8,128)(2,1)S(1)}, bf16[256,128]{1,0:T(8,128)(2,1)S(1)}, u32[]{:S(2)}, u32[]{:S(2)}) collective-permute-start(bf16[256,128]{1,0:T(8,128)(2,1)S(1)} %get-tuple-element.38), channel_id=1, source_target_pairs={{0,2},{2,0},{4,6},{6,4},{8,10},{10,8},{12,14},{14,12},{1,3},{3,1},... | collective-permute-start | bytes 196616 | tf_op jit(solution)/shard_map/ppermute | solution.py:643
  49.3 7.7 %encode.2 = (bf16[4,128,256]{2,1,0:T(8,128)(2,1)S(1)}, bf16[4,128,256]{2,1,0:T(8,128)(2,1)S(1)}) custom-call(s32[2]{0:T(128)S(1)} %pad_add_fusion.place, bf16[256,256]{1,0:T(8,128)(2,1)S(1)} %get-tuple-element.33.refs_0_, bf16[256,256]{1,0:T(8,128)(2,1)S(1)} %collective-permute-done.3.refs_1_, bf16[256,256]{1,0:T(8,128)(2,1)S(1)} %collective-permute-done.4.refs_2_, ...), custom_call_target="tpu_custom_call" | custom-call | flops 3221225472 | bytes 1048576 | tf_op jit(solution)/shard_map/encode/pallas_call | solution.py:438
  57.0 2.2 %collective-permute-start.19 = (bf16[4,128,256]{2,1,0:T(8,128)(2,1)S(1)}, bf16[4,128,256]{2,1,0:T(8,128)(2,1)S(1)}, u32[]{:S(2)}, u32[]{:S(2)}) collective-permute-start(bf16[4,128,256]{2,1,0:T(8,128)(2,1)S(1)} %get-tuple-element.56), channel_id=1, source_target_pairs={{0,8},{2,10},{4,12},{6,14},{8,0},{10,2},{12,4},{14,6},{1,9},{3,11}... | collective-permute-start | bytes 786440 | tf_op jit(solution)/shard_map/ppermute | solution.py:643
  59.2 7.7 %encode.3 = (bf16[256,256]{1,0:T(8,128)(2,1)S(1)}, bf16[256,256]{1,0:T(8,128)(2,1)S(1)}, bf16[256,256]{1,0:T(8,128)(2,1)S(1)}, bf16[256,256]{1,0:T(8,128)(2,1)S(...) custom-call(s32[2]{0:T(128)S(1)} %pad_add_fusion.place, ...), custom_call_target="tpu_custom_call" | custom-call | flops 3221225472 | bytes 1048576 | tf_op jit(solution)/shard_map/encode/pallas_call | solution.py:438
  67.0 1.4 %collective-permute-start.16 = (bf16[256,256]{1,0:T(8,128)(2,1)S(1)}, bf16[256,256]{1,0:T(8,128)(2,1)S(1)}, u32[]{:S(2)}, u32[]{:S(2)}) collective-permute-start(bf16[256,256]{1,0:T(8,128)(2,1)S(1)} %get-tuple-element.53), channel_id=1, source_target_pairs={{0,2},{2,0},{4,6},{6,4},{8,10},{10,8},{12,14},{14,12},{1,3},{3,1},... | collective-permute-start | bytes 393224 | tf_op jit(solution)/shard_map/ppermute | solution.py:643
  68.4 1.9 %collective-permute-start.17 = (bf16[256,256]{1,0:T(8,128)(2,1)S(1)}, bf16[256,256]{1,0:T(8,128)(2,1)S(1)}, u32[]{:S(2)}, u32[]{:S(2)}) collective-permute-start(bf16[256,256]{1,0:T(8,128)(2,1)S(1)} %get-tuple-element.54), channel_id=1, source_target_pairs={{0,4},{2,6},{4,0},{6,2},{8,12},{10,14},{12,8},{14,10},{1,5},{3,7},... | collective-permute-start | bytes 393224 | tf_op jit(solution)/shard_map/ppermute | solution.py:643
  70.6 1.4 %collective-permute-start.20 = (bf16[128,256]{1,0:T(8,128)(2,1)S(1)}, bf16[128,256]{1,0:T(8,128)(2,1)S(1)}, u32[]{:S(2)}, u32[]{:S(2)}) collective-permute-start(bf16[128,256]{1,0:T(8,128)(2,1)S(1)} %get-tuple-element.63), channel_id=1, source_target_pairs={{0,2},{2,0},{4,6},{6,4},{8,10},{10,8},{12,14},{14,12},{1,3},{3,1},... | collective-permute-start | bytes 196616 | tf_op jit(solution)/shard_map/ppermute | solution.py:643
  72.0 1.9 %collective-permute-start.21 = (bf16[128,256]{1,0:T(8,128)(2,1)S(1)}, bf16[128,256]{1,0:T(8,128)(2,1)S(1)}, u32[]{:S(2)}, u32[]{:S(2)}) collective-permute-start(bf16[128,256]{1,0:T(8,128)(2,1)S(1)} %get-tuple-element.62), channel_id=1, source_target_pairs={{0,4},{2,6},{4,0},{6,2},{8,12},{10,14},{12,8},{14,10},{1,5},{3,7},... | collective-permute-start | bytes 196616 | tf_op jit(solution)/shard_map/ppermute | solution.py:643
  74.0 2.5 %collective-permute-start.22 = (bf16[128,256]{1,0:T(8,128)(2,1)S(1)}, bf16[128,256]{1,0:T(8,128)(2,1)S(1)}, u32[]{:S(2)}, u32[]{:S(2)}) collective-permute-start(bf16[128,256]{1,0:T(8,128)(2,1)S(1)} %get-tuple-element.61), channel_id=1, source_target_pairs={{0,6},{2,4},{4,2},{6,0},{8,14},{10,12},{12,10},{14,8},{1,7},{3,5},... | collective-permute-start | bytes 196616 | tf_op jit(solution)/shard_map/ppermute | solution.py:643
  76.5 1.9 %collective-permute-done.18.refs_3_ = bf16[256,256]{1,0:T(8,128)(2,1)S(1)} collective-permute-done((bf16[256,256]{1,0:T(8,128)(2,1)S(1)}, bf16[256,256]{1,0:T(8,128)(2,1)S(1)}, u32[]{:S(2)}, u32[]{:S(2)}) %collective-permute-start.18) | collective-permute-done | bytes 131104 | tf_op jit(solution)/shard_map/ppermute | solution.py:643
  79.3 2.7 %collective-permute-start.26 = (bf16[128,256]{1,0:T(8,128)(2,1)S(1)}, bf16[128,256]{1,0:T(8,128)(2,1)S(1)}, u32[]{:S(2)}, u32[]{:S(2)}) collective-permute-start(bf16[128,256]{1,0:T(8,128)(2,1)S(1)} %get-tuple-element.59), channel_id=1, source_target_pairs={{0,12},{2,14},{4,8},{6,10},{8,4},{10,6},{12,0},{14,2},{1,13},{3,15... | collective-permute-start | bytes 196616 | tf_op jit(solution)/shard_map/ppermute | solution.py:643
  82.0 2.1 %collective-permute-start.27 = (bf16[128,256]{1,0:T(8,128)(2,1)S(1)}, bf16[128,256]{1,0:T(8,128)(2,1)S(1)}, u32[]{:S(2)}, u32[]{:S(2)}) collective-permute-start(bf16[128,256]{1,0:T(8,128)(2,1)S(1)} %get-tuple-element.60), channel_id=1, source_target_pairs={{0,14},{2,12},{4,10},{6,8},{8,6},{10,4},{12,2},{14,0},{1,15},{3,13... | collective-permute-start | bytes 196616 | tf_op jit(solution)/shard_map/ppermute | solution.py:643
  84.9 2.2 %convolve.2.refs_13_ = bf16[2048,256]{1,0:T(8,128)(2,1)} custom-call(s32[2]{0:T(128)S(1)} %pad_add_fusion.place, bf16[64,256]{1,0:T(8,128)(2,1)S(1)} %broadcast_in_dim.3.top.bottom, bf16[64,256]{1,0:T(8,128)(2,1)S(1)} %broadcast_in_dim.3.top.bottom, bf16[256,256]{1,0:T(8,128)(2,1)S(1)} %get-tuple-element.52.refs_0_, ...), custom_call_target="tpu_custom_call" | custom-call | flops 603979776 | bytes 524288 | tf_op jit(solution)/shard_map/convolve/pallas_call | solution.py:580
  87.6 1.5 %collective-permute-done.27.refs_11_ = bf16[128,256]{1,0:T(8,128)(2,1)S(1)} collective-permute-done((bf16[128,256]{1,0:T(8,128)(2,1)S(1)}, bf16[128,256]{1,0:T(8,128)(2,1)S(1)}, u32[]{:S(2)}, u32[]{:S(2)}) %collective-permute-start.27) | collective-permute-done | bytes 65568 | tf_op jit(solution)/shard_map/ppermute | solution.py:643
  89.1 4.3 %convolve.3 = bf16[2048,256]{1,0:T(8,128)(2,1)} custom-call(s32[2]{0:T(128)S(1)} %pad_add_fusion.place, bf16[64,256]{1,0:T(8,128)(2,1)S(1)} %collective-permute-done.23.top.bottom, bf16[64,256]{1,0:T(8,128)(2,1)S(1)} %collective-permute-done.23.top.bottom, bf16[256,256]{1,0:T(8,128)(2,1)S(1)} %get-tuple-element.52.refs_0_, ...), custom_call_target="tpu_custom_call", output_to_operand_aliasing={{}: (16, {})} | custom-call | flops 1811939328 | bytes 1572864 | tf_op jit(solution)/shard_map/convolve/pallas_call | solution.py:580
  (66 shorter events, 13.3 us)
Async XLA Ops:
  0.0 16.2 %collective-permute-start.6 = (bf16[512,256]{1,0:T(8,128)(2,1)}, bf16[512,256]{1,0:T(8,128)(2,1)S(1)}, u32[]{:S(2)}, u32[]{:S(2)}) collective-permute-start(bf16[512,256]{1,0:T(8,128)(2,1)} %bitcast.17), channel_id=1, source_target_pairs={{0,8},{2,10},{4,12},{6,14},{8,0},{10,2},{12,4},{14,6},{1,9},{3,11}... | collective-permute-start | bytes 786440 | tf_op jit(solution)/shard_map/ppermute | solution.py:643
  4.1 14.1 %collective-permute-start = (bf16[512,256]{1,0:T(8,128)(2,1)}, bf16[512,256]{1,0:T(8,128)(2,1)S(1)}, u32[]{:S(2)}, u32[]{:S(2)}) collective-permute-start(bf16[512,256]{1,0:T(8,128)(2,1)} %bitcast.18), channel_id=1, source_target_pairs={{0,1},{1,0},{2,3},{3,2},{4,5},{5,4},{6,7},{7,6},{8,9},{9,8},{10,11... | collective-permute-start | bytes 786440 | tf_op jit(solution)/shard_map/ppermute | solution.py:637
  16.2 23.3 %collective-permute-start.7 = (bf16[512,256]{1,0:T(8,128)(2,1)S(1)}, bf16[512,256]{1,0:T(8,128)(2,1)S(1)}, u32[]{:S(2)}, u32[]{:S(2)}) collective-permute-start(bf16[512,256]{1,0:T(8,128)(2,1)S(1)} %collective-permute-done.6.refs_0_), channel_id=1, source_target_pairs={{0,1},{1,0},{2,3},{3,2},{4,5},{5,4},{6,7},{7,6},{8,9},{9,8},{10,11... | collective-permute-start | bytes 786440 | tf_op jit(solution)/shard_map/ppermute | solution.py:637
  26.2 16.6 %collective-permute-start.3 = (bf16[256,256]{1,0:T(8,128)(2,1)S(1)}, bf16[256,256]{1,0:T(8,128)(2,1)S(1)}, u32[]{:S(2)}, u32[]{:S(2)}) collective-permute-start(bf16[256,256]{1,0:T(8,128)(2,1)S(1)} %get-tuple-element.34), channel_id=1, source_target_pairs={{0,2},{2,0},{4,6},{6,4},{8,10},{10,8},{12,14},{14,12},{1,3},{3,1},... | collective-permute-start | bytes 393224 | tf_op jit(solution)/shard_map/ppermute | solution.py:643
  27.9 4.9 %collective-permute-start.8 = (f32[16,512]{1,0:T(8,128)S(1)}, f32[16,512]{1,0:T(8,128)S(1)}, u32[]{:S(2)}, u32[]{:S(2)}) collective-permute-start(f32[16,512]{1,0:T(8,128)S(1)} %bitcast.22), channel_id=1, source_target_pairs={{0,8},{2,10},{4,12},{6,14},{8,0},{10,2},{12,4},{14,6},{1,9},{3,11}... | collective-permute-start | bytes 98312 | tf_op jit(solution)/shard_map/ppermute | solution.py:643
  32.8 12.9 %collective-permute-start.4 = (bf16[256,256]{1,0:T(8,128)(2,1)S(1)}, bf16[256,256]{1,0:T(8,128)(2,1)S(1)}, u32[]{:S(2)}, u32[]{:S(2)}) collective-permute-start(bf16[256,256]{1,0:T(8,128)(2,1)S(1)} %get-tuple-element.35), channel_id=1, source_target_pairs={{0,4},{2,6},{4,0},{6,2},{8,12},{10,14},{12,8},{14,10},{1,5},{3,7},... | collective-permute-start | bytes 393224 | tf_op jit(solution)/shard_map/ppermute | solution.py:643
  33.8 13.5 %collective-permute-start.5 = (bf16[256,256]{1,0:T(8,128)(2,1)S(1)}, bf16[256,256]{1,0:T(8,128)(2,1)S(1)}, u32[]{:S(2)}, u32[]{:S(2)}) collective-permute-start(bf16[256,256]{1,0:T(8,128)(2,1)S(1)} %get-tuple-element.36), channel_id=1, source_target_pairs={{0,6},{2,4},{4,2},{6,0},{8,14},{10,12},{12,10},{14,8},{1,7},{3,5},... | collective-permute-start | bytes 393224 | tf_op jit(solution)/shard_map/ppermute | solution.py:643
  40.2 8.1 %collective-permute-start.13 = (bf16[256,128]{1,0:T(8,128)(2,1)S(1)}, bf16[256,128]{1,0:T(8,128)(2,1)S(1)}, u32[]{:S(2)}, u32[]{:S(2)}) collective-permute-start(bf16[256,128]{1,0:T(8,128)(2,1)S(1)} %get-tuple-element.48), channel_id=1, source_target_pairs={{0,2},{2,0},{4,6},{6,4},{8,10},{10,8},{12,14},{14,12},{1,3},{3,1},... | collective-permute-start | bytes 196616 | tf_op jit(solution)/shard_map/ppermute | solution.py:643
  41.8 7.4 %collective-permute-start.14 = (bf16[256,128]{1,0:T(8,128)(2,1)S(1)}, bf16[256,128]{1,0:T(8,128)(2,1)S(1)}, u32[]{:S(2)}, u32[]{:S(2)}) collective-permute-start(bf16[256,128]{1,0:T(8,128)(2,1)S(1)} %get-tuple-element.49), channel_id=1, source_target_pairs={{0,4},{2,6},{4,0},{6,2},{8,12},{10,14},{12,8},{14,10},{1,5},{3,7},... | collective-permute-start | bytes 196616 | tf_op jit(solution)/shard_map/ppermute | solution.py:643
  42.9 6.4 %collective-permute-start.15 = (bf16[256,128]{1,0:T(8,128)(2,1)S(1)}, bf16[256,128]{1,0:T(8,128)(2,1)S(1)}, u32[]{:S(2)}, u32[]{:S(2)}) collective-permute-start(bf16[256,128]{1,0:T(8,128)(2,1)S(1)} %get-tuple-element.50), channel_id=1, source_target_pairs={{0,6},{2,4},{4,2},{6,0},{8,14},{10,12},{12,10},{14,8},{1,7},{3,5},... | collective-permute-start | bytes 196616 | tf_op jit(solution)/shard_map/ppermute | solution.py:643
  45.7 13.5 %collective-permute-start.10 = (bf16[256,128]{1,0:T(8,128)(2,1)S(1)}, bf16[256,128]{1,0:T(8,128)(2,1)S(1)}, u32[]{:S(2)}, u32[]{:S(2)}) collective-permute-start(bf16[256,128]{1,0:T(8,128)(2,1)S(1)} %get-tuple-element.38), channel_id=1, source_target_pairs={{0,2},{2,0},{4,6},{6,4},{8,10},{10,8},{12,14},{14,12},{1,3},{3,1},... | collective-permute-start | bytes 196616 | tf_op jit(solution)/shard_map/ppermute | solution.py:643
  47.3 11.9 %collective-permute-start.11 = (bf16[256,128]{1,0:T(8,128)(2,1)S(1)}, bf16[256,128]{1,0:T(8,128)(2,1)S(1)}, u32[]{:S(2)}, u32[]{:S(2)}) collective-permute-start(bf16[256,128]{1,0:T(8,128)(2,1)S(1)} %get-tuple-element.39), channel_id=1, source_target_pairs={{0,4},{2,6},{4,0},{6,2},{8,12},{10,14},{12,8},{14,10},{1,5},{3,7},... | collective-permute-start | bytes 196616 | tf_op jit(solution)/shard_map/ppermute | solution.py:643
  48.3 10.9 %collective-permute-start.12 = (bf16[256,128]{1,0:T(8,128)(2,1)S(1)}, bf16[256,128]{1,0:T(8,128)(2,1)S(1)}, u32[]{:S(2)}, u32[]{:S(2)}) collective-permute-start(bf16[256,128]{1,0:T(8,128)(2,1)S(1)} %get-tuple-element.40), channel_id=1, source_target_pairs={{0,6},{2,4},{4,2},{6,0},{8,14},{10,12},{12,10},{14,8},{1,7},{3,5},... | collective-permute-start | bytes 196616 | tf_op jit(solution)/shard_map/ppermute | solution.py:643
  57.0 13.5 %collective-permute-start.19 = (bf16[4,128,256]{2,1,0:T(8,128)(2,1)S(1)}, bf16[4,128,256]{2,1,0:T(8,128)(2,1)S(1)}, u32[]{:S(2)}, u32[]{:S(2)}) collective-permute-start(bf16[4,128,256]{2,1,0:T(8,128)(2,1)S(1)} %get-tuple-element.56), channel_id=1, source_target_pairs={{0,8},{2,10},{4,12},{6,14},{8,0},{10,2},{12,4},{14,6},{1,9},{3,11}... | collective-permute-start | bytes 786440 | tf_op jit(solution)/shard_map/ppermute | solution.py:643
  67.0 7.0 %collective-permute-start.16 = (bf16[256,256]{1,0:T(8,128)(2,1)S(1)}, bf16[256,256]{1,0:T(8,128)(2,1)S(1)}, u32[]{:S(2)}, u32[]{:S(2)}) collective-permute-start(bf16[256,256]{1,0:T(8,128)(2,1)S(1)} %get-tuple-element.53), channel_id=1, source_target_pairs={{0,2},{2,0},{4,6},{6,4},{8,10},{10,8},{12,14},{14,12},{1,3},{3,1},... | collective-permute-start | bytes 393224 | tf_op jit(solution)/shard_map/ppermute | solution.py:643
  68.4 8.1 %collective-permute-start.17 = (bf16[256,256]{1,0:T(8,128)(2,1)S(1)}, bf16[256,256]{1,0:T(8,128)(2,1)S(1)}, u32[]{:S(2)}, u32[]{:S(2)}) collective-permute-start(bf16[256,256]{1,0:T(8,128)(2,1)S(1)} %get-tuple-element.54), channel_id=1, source_target_pairs={{0,4},{2,6},{4,0},{6,2},{8,12},{10,14},{12,8},{14,10},{1,5},{3,7},... | collective-permute-start | bytes 393224 | tf_op jit(solution)/shard_map/ppermute | solution.py:643
  70.4 8.0 %collective-permute-start.18 = (bf16[256,256]{1,0:T(8,128)(2,1)S(1)}, bf16[256,256]{1,0:T(8,128)(2,1)S(1)}, u32[]{:S(2)}, u32[]{:S(2)}) collective-permute-start(bf16[256,256]{1,0:T(8,128)(2,1)S(1)} %get-tuple-element.55), channel_id=1, source_target_pairs={{0,6},{2,4},{4,2},{6,0},{8,14},{10,12},{12,10},{14,8},{1,7},{3,5},... | collective-permute-start | bytes 393224 | tf_op jit(solution)/shard_map/ppermute | solution.py:643
  70.6 8.8 %collective-permute-start.20 = (bf16[128,256]{1,0:T(8,128)(2,1)S(1)}, bf16[128,256]{1,0:T(8,128)(2,1)S(1)}, u32[]{:S(2)}, u32[]{:S(2)}) collective-permute-start(bf16[128,256]{1,0:T(8,128)(2,1)S(1)} %get-tuple-element.63), channel_id=1, source_target_pairs={{0,2},{2,0},{4,6},{6,4},{8,10},{10,8},{12,14},{14,12},{1,3},{3,1},... | collective-permute-start | bytes 196616 | tf_op jit(solution)/shard_map/ppermute | solution.py:643
  72.0 10.0 %collective-permute-start.21 = (bf16[128,256]{1,0:T(8,128)(2,1)S(1)}, bf16[128,256]{1,0:T(8,128)(2,1)S(1)}, u32[]{:S(2)}, u32[]{:S(2)}) collective-permute-start(bf16[128,256]{1,0:T(8,128)(2,1)S(1)} %get-tuple-element.62), channel_id=1, source_target_pairs={{0,4},{2,6},{4,0},{6,2},{8,12},{10,14},{12,8},{14,10},{1,5},{3,7},... | collective-permute-start | bytes 196616 | tf_op jit(solution)/shard_map/ppermute | solution.py:643
  74.0 10.2 %collective-permute-start.22 = (bf16[128,256]{1,0:T(8,128)(2,1)S(1)}, bf16[128,256]{1,0:T(8,128)(2,1)S(1)}, u32[]{:S(2)}, u32[]{:S(2)}) collective-permute-start(bf16[128,256]{1,0:T(8,128)(2,1)S(1)} %get-tuple-element.61), channel_id=1, source_target_pairs={{0,6},{2,4},{4,2},{6,0},{8,14},{10,12},{12,10},{14,8},{1,7},{3,5},... | collective-permute-start | bytes 196616 | tf_op jit(solution)/shard_map/ppermute | solution.py:643
  76.5 10.7 %collective-permute-start.24 = (bf16[128,256]{1,0:T(8,128)(2,1)S(1)}, bf16[128,256]{1,0:T(8,128)(2,1)S(1)}, u32[]{:S(2)}, u32[]{:S(2)}) collective-permute-start(bf16[128,256]{1,0:T(8,128)(2,1)S(1)} %get-tuple-element.57), channel_id=1, source_target_pairs={{0,8},{2,10},{4,12},{6,14},{8,0},{10,2},{12,4},{14,6},{1,9},{3,11}... | collective-permute-start | bytes 196616 | tf_op jit(solution)/shard_map/ppermute | solution.py:643
  78.4 9.2 %collective-permute-start.25 = (bf16[128,256]{1,0:T(8,128)(2,1)S(1)}, bf16[128,256]{1,0:T(8,128)(2,1)S(1)}, u32[]{:S(2)}, u32[]{:S(2)}) collective-permute-start(bf16[128,256]{1,0:T(8,128)(2,1)S(1)} %get-tuple-element.58), channel_id=1, source_target_pairs={{0,10},{2,8},{4,14},{6,12},{8,2},{10,0},{12,6},{14,4},{1,11},{3,9}... | collective-permute-start | bytes 196616 | tf_op jit(solution)/shard_map/ppermute | solution.py:643
  79.3 8.3 %collective-permute-start.26 = (bf16[128,256]{1,0:T(8,128)(2,1)S(1)}, bf16[128,256]{1,0:T(8,128)(2,1)S(1)}, u32[]{:S(2)}, u32[]{:S(2)}) collective-permute-start(bf16[128,256]{1,0:T(8,128)(2,1)S(1)} %get-tuple-element.59), channel_id=1, source_target_pairs={{0,12},{2,14},{4,8},{6,10},{8,4},{10,6},{12,0},{14,2},{1,13},{3,15... | collective-permute-start | bytes 196616 | tf_op jit(solution)/shard_map/ppermute | solution.py:643
  82.0 7.1 %collective-permute-start.27 = (bf16[128,256]{1,0:T(8,128)(2,1)S(1)}, bf16[128,256]{1,0:T(8,128)(2,1)S(1)}, u32[]{:S(2)}, u32[]{:S(2)}) collective-permute-start(bf16[128,256]{1,0:T(8,128)(2,1)S(1)} %get-tuple-element.60), channel_id=1, source_target_pairs={{0,14},{2,12},{4,10},{6,8},{8,6},{10,4},{12,2},{14,0},{1,15},{3,13... | collective-permute-start | bytes 196616 | tf_op jit(solution)/shard_map/ppermute | solution.py:643
  (15 other events, 94.7 us)
